TPU v7x, 16 devices: a whole 2x2x2 slice. The times are simulated.
16 devices in a mesh: dp: 2 (over z), fo: 2 (over y), fi: 4 (over x, core).
Axes of the slice: x: 2, y: 2, z: 2, core: 2. Of those that a mesh axis runs over, the one named last changes fastest.
Arguments:
- X: bfloat16 [65536, 576], P(('dp', 'fo', 'fi'))
- dY: bfloat16 [65536, 576], P(('dp', 'fo', 'fi'))
- W1: bfloat16 [576, 1536], P(None, ('fo', 'fi'))
- W3: bfloat16 [576, 1536], P(None, ('fo', 'fi'))
- W2: bfloat16 [1536, 576], P(('fo', 'fi'))
- G: float32 [16, 3, 576, 1536], P(('dp', 'fo', 'fi'))
Outputs:
- output 1: bfloat16 [65536, 576], P(('dp', 'fo', 'fi'))
- output 2: float32 [3, 576, 1536], P(None, None, ('fo', 'fi'))
- output 3: float32 [16, 3, 576, 1536], P(('dp', 'fo', 'fi'))
All inputs are finite; a program needn't handle non-finite values.
Results may differ from a plain program's by a relative error of at most 0.0105754.
Values are sent between devices in bfloat16 or wider.
A program may use at most 1 GiB of HBM per device.

v0:
```python
import jax
import jax.numpy as jnp
from jax import lax
from jax.sharding import PartitionSpec as P


def mlp_grads(x, dy, w1, w3, w2t):
    a = jnp.dot(x, w1, preferred_element_type=jnp.float32)
    b = jnp.dot(x, w3, preferred_element_type=jnp.float32)
    s = jax.nn.sigmoid(a)
    sa = a * s
    h = (sa * b).astype(jnp.bfloat16)
    dh = jnp.dot(dy, w2t, preferred_element_type=jnp.float32)
    da = (dh * b * (s * (1.0 + a * (1.0 - s)))).astype(jnp.bfloat16)
    db = (dh * sa).astype(jnp.bfloat16)
    dx = (jnp.dot(da, w1.T, preferred_element_type=jnp.float32)
          + jnp.dot(db, w3.T, preferred_element_type=jnp.float32)).astype(jnp.bfloat16)
    gw1 = jnp.dot(x.T, da, preferred_element_type=jnp.float32)
    gw3 = jnp.dot(x.T, db, preferred_element_type=jnp.float32)
    gw2 = jnp.dot(dy.T, h, preferred_element_type=jnp.float32)
    return dx, jnp.stack([gw1, gw3, gw2])


def solution(mesh):
    grp = ("fo", "fi")
    alla = ("dp", "fo", "fi")

    def local(x, dy, w1s, w3s, w2s, g):
        w1 = lax.all_gather(w1s, grp, axis=1, tiled=True)
        w3 = lax.all_gather(w3s, grp, axis=1, tiled=True)
        w2 = lax.all_gather(w2s, grp, axis=0, tiled=True)
        gs = lax.psum_scatter(g[0].astype(jnp.bfloat16), grp, scatter_dimension=2, tiled=True)
        dwn = lax.psum(gs.astype(jnp.float32), "dp")
        dx, dwl = mlp_grads(x, dy, w1, w3, w2.T)
        return dx, dwn, dwl[None]

    return jax.shard_map(
        local, mesh=mesh,
        in_specs=(P(alla, None), P(alla, None), P(None, grp), P(None, grp), P(grp, None),
                  P(alla, None, None, None)),
        out_specs=(P(alla, None), P(None, None, grp), P(alla, None, None, None)),
        check_vma=False)
```

profile of v0, /device:TPU:0, one launch (start us, length us, event | category | flops | bytes accessed | tf_op | source)
XLA Modules:
  0.0 233.1 jit_solution(2957616309564379687)
XLA Ops:
  7.2 0.0 all-gather.6.cloned.1.call-start
  7.2 0.7 all-gather.6.cloned.1.call-update
  7.9 0.0 all-gather.8.cloned.1.call-start
  7.9 0.7 all-gather.8.cloned.1.call-update
  8.6 0.0 all-gather.4.cloned.1.call-start
  8.7 0.7 all-gather.4.cloned.1.call-update
  9.4 0.0 reduce-scatter.2.cloned.1.call-start
  9.4 10.5 %copy.9 = bf16[1,3,576,1536]{2,3,1,0:T(8,128)(2,1)} copy(f32[1,3,576,1536]{3,2,1,0:T(8,128)} %param.11) | data formatting | bytes 15925248 | tf_op args[5]
  19.9 0.0 reduce-scatter.2.cloned.1.call-update
  19.9 15.9 %all-gather.6.cloned.1.call-done = bf16[576,1536]{0,1:T(8,128)(2,1)} async-done(((bf16[576,192]{0,1:T(8,128)(2,1)}), bf16[576,1536]{0,1:T(8,128)(2,1)}) %all-gather.6.cloned.1.call-update) | async-done | bytes 1769488 | tf_op jit(solution)/shard_map/all_gather | solution.py:30
  35.9 17.7 %fusion.5 = f32[4096,1536]{1,0:T(8,128)} fusion(bf16[4096,576]{0,1:T(8,128)(2,1)} %param.6, bf16[576,1536]{0,1:T(8,128)(2,1)} %all-gather.6.cloned.1.call-done), kind=kOutput, calls=%fused_computation.13 | convolution fusion | flops 7247757312 | bytes 31653888 | tf_op jit(solution)/shard_map/dot_general | solution.py:9
  53.6 7.3 %all-gather.8.cloned.1.call-done = bf16[576,1536]{0,1:T(8,128)(2,1)} async-done(((bf16[576,192]{0,1:T(8,128)(2,1)}), bf16[576,1536]{0,1:T(8,128)(2,1)}) %all-gather.8.cloned.1.call-update) | async-done | bytes 1769488 | tf_op jit(solution)/shard_map/all_gather | solution.py:29
  61.0 17.8 %fusion.6 = f32[4096,1536]{1,0:T(8,128)} fusion(bf16[4096,576]{0,1:T(8,128)(2,1)} %param.6, bf16[576,1536]{0,1:T(8,128)(2,1)} %all-gather.8.cloned.1.call-done), kind=kOutput, calls=%fused_computation.14 | convolution fusion | flops 7247757312 | bytes 31653888 | tf_op jit(solution)/shard_map/dot_general | solution.py:8
  78.8 19.7 %fusion.3 = f32[1,576,1536]{2,1,0:T(8,128)S(1)} fusion(bf16[4096,576]{0,1:T(8,128)(2,1)} %param.7, f32[4096,1536]{1,0:T(8,128)} %fusion.5, f32[4096,1536]{1,0:T(8,128)} %fusion.6), kind=kOutput, calls=%fused_computation.9 | convolution fusion | flops 7285506048 | bytes 58589184 | tf_op jit(solution)/shard_map/dot_general | solution.py:20
  98.5 0.0 all-gather.4.cloned.1.call-done
  98.5 34.2 %multiply_convert_fusion.1 = (bf16[4096,1536]{1,0:T(8,128)(2,1)}, bf16[4096,1536]{1,0:T(8,128)(2,1)}) fusion(f32[4096,1536]{1,0:T(8,128)} %fusion.6, f32[4096,1536]{1,0:T(8,128)} %fusion.5, bf16[4096,576]{0,1:T(8,128)(2,1)} %param.7, bf16[1536,576]{1,0:T(8,128)(2,1)} %all-gather.4.cloned.1.call-done), kind=kOutput, calls=%fused_computation.1 | convolution fusion | flops 7329546240 | bytes 81985536 | tf_op jit(solution)/shard_map/dot_general | solution.py:13
  132.7 0.0 copy-start.1
  132.7 11.9 %convolution_bitcast_fusion = f32[1,576,1536]{2,1,0:T(8,128)S(1)} fusion(bf16[4096,576]{0,1:T(8,128)(2,1)} %param.6, bf16[4096,1536]{1,0:T(8,128)(2,1)} %get-tuple-element.3), kind=kOutput, calls=%fused_computation.10 | convolution fusion | flops 7247757312 | bytes 20840448 | tf_op jit(solution)/shard_map/dot_general | solution.py:19
  144.6 0.0 copy-done.1
  144.6 9.5 %convolution_bitcast_fusion.1 = f32[1,576,1536]{2,1,0:T(8,128)S(1)} fusion(bf16[4096,576]{0,1:T(8,128)(2,1)} %param.6, bf16[4096,1536]{1,0:T(8,128)(2,1)S(1)} %copy-done.1), kind=kOutput, calls=%fused_computation.11 | convolution fusion | flops 7247757312 | bytes 20840448 | tf_op jit(solution)/shard_map/dot_general | solution.py:18
  154.2 5.1 %maximum_bitcast_fusion = f32[1,3,576,1536]{3,2,1,0:T(8,128)} fusion(f32[1,576,1536]{2,1,0:T(8,128)S(1)} %fusion.3, f32[1,576,1536]{2,1,0:T(8,128)S(1)} %convolution_bitcast_fusion, f32[1,576,1536]{2,1,0:T(8,128)S(1)} %convolution_bitcast_fusion.1), kind=kLoop, calls=%fused_computation.6 | loop fusion | flops 5308416 | bytes 21233664 | tf_op jit(solution)/shard_map/broadcast_in_dim | solution.py:35
  159.3 0.0 copy-start
  159.3 13.5 %fusion.7 = f32[4096,576]{0,1:T(8,128)} fusion(bf16[4096,1536]{1,0:T(8,128)(2,1)} %get-tuple-element.4, bf16[576,1536]{0,1:T(8,128)(2,1)} %all-gather.8.cloned.1.call-done), kind=kOutput, calls=%fused_computation.15 | convolution fusion | flops 7247757312 | bytes 23789568 | tf_op jit(solution)/shard_map/dot_general | solution.py:16
  172.8 0.0 copy-done
  172.8 13.5 %add_convert_fusion = bf16[4096,576]{0,1:T(8,128)(2,1)} fusion(f32[4096,576]{0,1:T(8,128)} %fusion.7, bf16[4096,1536]{1,0:T(8,128)(2,1)} %get-tuple-element.3, bf16[576,1536]{0,1:T(8,128)(2,1)S(1)} %copy-done), kind=kOutput, calls=%fused_computation.7 | convolution fusion | flops 7252475904 | bytes 28508160 | tf_op jit(solution)/shard_map/dot_general | solution.py:17
  186.2 0.0 reduce-scatter.2.cloned.1.call-done
  186.2 40.4 %all-reduce.1 = f32[3,576,192]{1,2,0:T(8,128)} all-reduce(bf16[3,576,192]{1,2,0:T(8,128)(2,1)} %reduce-scatter.2.cloned.1.call-done), channel_id=1, replica_groups=mesh['dp'=2,'fo'=2,'fi'=4] {'dp'}, use_global_device_ids=true, to_apply=%region_1.0 | all-reduce | flops 331776 | bytes 1990656 | tf_op jit(solution)/shard_map/psum | solution.py:33
Async XLA Ops:
  7.2 28.7 %all-gather.6.cloned.1.call-start = ((), (), s32[]{:S(2)}) async-start(), calls=%async_computation.2 | async-start | bytes 2211840 | tf_op jit(solution)/shard_map/all_gather | solution.py:30
  7.9 53.1 %all-gather.8.cloned.1.call-start = ((), (), s32[]{:S(2)}) async-start(), calls=%async_computation.3 | async-start | bytes 2211840 | tf_op jit(solution)/shard_map/all_gather | solution.py:29
  8.6 89.9 %all-gather.4.cloned.1.call-start = ((), (), s32[]{:S(2)}) async-start(), calls=%async_computation.1 | async-start | bytes 2211840 | tf_op jit(solution)/shard_map/all_gather | solution.py:31
  9.4 176.8 %reduce-scatter.2.cloned.1.call-start = ((), (), s32[]{:S(2)}) async-start(), calls=%async_computation.4 | async-start | bytes 6635520 | tf_op jit(solution)/shard_map/reduce_scatter | solution.py:32
  132.7 11.9 %copy-start.1 = (bf16[4096,1536]{1,0:T(8,128)(2,1)S(1)}, bf16[4096,1536]{1,0:T(8,128)(2,1)}, u32[]{:S(2)}) copy-start(bf16[4096,1536]{1,0:T(8,128)(2,1)} %get-tuple-element.4) | copy-start | bytes 37748740
  159.3 13.5 %copy-start = (bf16[576,1536]{0,1:T(8,128)(2,1)S(1)}, bf16[576,1536]{0,1:T(8,128)(2,1)}, u32[]{:S(2)}) copy-start(bf16[576,1536]{0,1:T(8,128)(2,1)} %all-gather.6.cloned.1.call-done) | copy-start | bytes 5308420
Sparse Core Ops, SparseCore 0:
  9.8 26.0 all-gather.5
  37.7 23.1 all-gather.7
  62.8 23.1 all-gather.3
  89.3 53.3 reduce-scatter.1
where the time goes:
time: 234 us; the launch traced here: 233 us
  matrix products  138 us (59%)
  blocking collectives  40.4 us (17%)
  waiting for transfers between devices  25.4 us (11%)
  between operations  13.8 us (6%)
  local copies, waits for them, and re-layouts  10.5 us (4%)
  other arithmetic  5.13 us (2%)
    psum x1, blocking collectives, local(): dwn = lax.psum(gs.astype(jnp.float32), 'dp')  40.4 us
    dot_general x1, matrix products, mlp_grads(): dh = jnp.dot(dy, w2t, preferred_element_type=jnp.float32)  34.2 us
    dot_general x1, matrix products, mlp_grads(): gw2 = jnp.dot(dy.T, h, preferred_element_type=jnp.float32)  19.7 us
    dot_general x1, matrix products, mlp_grads(): a = jnp.dot(x, w1, preferred_element_type=jnp.float32)  17.8 us
    dot_general x1, matrix products, mlp_grads(): b = jnp.dot(x, w3, preferred_element_type=jnp.float32)  17.7 us
    all_gather x1, waiting for transfers between devices, local(): w3 = lax.all_gather(w3s, grp, axis=1, tiled=True)  15.9 us
    dot_general x1, matrix products, mlp_grads(): jnp.dot(da, w1.T, preferred_element_type=jnp.float32)  13.5 us
    dot_general x1, matrix products, mlp_grads(): jnp.dot(db, w3.T, preferred_element_type=jnp.float32)  13.5 us
  transfers between devices with their start and end apart: 4, of which 2 were waited for; matrix products, arithmetic and copies ran while one was open for 66% of the time, Pallas kernels for 0%

commit v1 on v0

v1 whole, which is shorter than its diff:
```python
import jax
import jax.numpy as jnp
from jax import lax
from jax.experimental import pallas as pl
from jax.experimental.pallas import tpu as pltpu
from jax.sharding import PartitionSpec as P

bf16, f32 = jnp.bfloat16, jnp.float32
T, D, F = 4096, 576, 1536
FB, TB, RC = 384, 512, 16
NF, NT = F // FB, T // TB
NN = (((1,), (0,)), ((), ()))
NTD = (((1,), (1,)), ((), ()))
ANY = pl.BlockSpec(memory_space=pl.ANY)
VM = pl.BlockSpec(memory_space=pltpu.VMEM)


def dot(a, b):
    return lax.dot_general(a, b, NN, preferred_element_type=f32)


def kernel_a(x_hbm, dy_hbm, w_ref, wd_ref, dx_hbm, r_hbm,
             x, dy, acts, dd, hh, dxa, dxo, sx, sd, so, sdx):
    def xcp(t):
        return pltpu.make_async_copy(x_hbm.at[:, pl.ds(t * TB, TB)], x.at[t], sx.at[t])

    def dcp(t):
        return pltpu.make_async_copy(dy_hbm.at[:, pl.ds(t * TB, TB)], dy.at[t], sd.at[t])

    for t in range(NT):
        xcp(t).start()
        dcp(t).start()
    dd[1] = jnp.zeros(dd.shape[1:], bf16)

    def outcp(s, p):
        ts = pl.ds(pl.multiple_of(s % NT * TB, TB), TB)
        fs = pl.ds(pl.multiple_of(s // NT * FB, FB), FB)
        return [pltpu.make_async_copy(dd.at[p, pl.ds(0, FB)], r_hbm.at[0, fs, ts], so.at[p, 0]),
                pltpu.make_async_copy(dd.at[p, pl.ds(FB, FB)], r_hbm.at[1, fs, ts], so.at[p, 1]),
                pltpu.make_async_copy(hh.at[p], r_hbm.at[2, fs, ts], so.at[p, 2])]

    def fwd(f, t, p):
        fs = pl.ds(pl.multiple_of(f * FB, FB), FB)
        acts[p, 0] = dot(w_ref[0, fs, :], x[t])
        acts[p, 1] = dot(w_ref[1, fs, :], x[t])
        acts[p, 2] = dot(w_ref[2, fs, :], dy[t])

    def ew(p):
        for r in range(0, FB, RC):
            a, b, dh = (acts[p, k, r:r + RC, :] for k in range(3))
            s = 0.5 * jnp.tanh(0.5 * a) + 0.5
            sa = a * s
            hh[p, r:r + RC, :] = (sa * b).astype(bf16)
            dd[p, r:r + RC, :] = (dh * b * (s * (1.0 + a * (1.0 - s)))).astype(bf16)
            dd[p, FB + r:FB + r + RC, :] = (dh * sa).astype(bf16)

    def dxp(s, p):
        f, t = s // NT, s % NT
        dxa[t] = jnp.where(f == 0, 0.0, dxa[t]) + dot(wd_ref[f], dd[p])

    def body(i, c):
        s0 = 2 * i
        f, t0 = s0 // NT, s0 % NT
        s1, t1 = s0 + 1, t0 + 1

        @pl.when(f == 0)
        def _():
            for t in (t0, t1):
                xcp(t).wait()
                dcp(t).wait()

        @pl.when(i > 0)
        def _():
            for cp in outcp(s0 - 2, 0):
                cp.wait()

        fwd(f, t0, 0)
        ew(0)
        dxp(jnp.maximum(s0 - 1, 0), 1)

        @pl.when(i > 0)
        def _():
            for cp in outcp(s0 - 1, 1):
                cp.wait()

        for cp in outcp(s0, 0):
            cp.start()
        fwd(f, t1, 1)
        ew(1)
        dxp(s0, 0)
        for cp in outcp(s1, 1):
            cp.start()
        return c

    n = NF * NT
    lax.fori_loop(0, n // 2, body, 0)
    dxp(n - 1, 1)
    for p in (0, 1):
        for cp in outcp(n - 2 + p, p):
            cp.wait()

    def ocp(t, p):
        return pltpu.make_async_copy(dxo.at[p], dx_hbm.at[:, pl.ds(t * TB, TB)], sdx.at[p])

    for t in range(NT):
        p = t % 2
        if t >= 2:
            ocp(t - 2, p).wait()
        dxo[p] = dxa[t].astype(bf16)
        ocp(t, p).start()
    ocp(NT - 2, 0).wait()
    ocp(NT - 1, 1).wait()


def call_a(x, dy, w, wd):
    return pl.pallas_call(
        kernel_a,
        out_shape=(jax.ShapeDtypeStruct((D, T), bf16), jax.ShapeDtypeStruct((3, F, T), bf16)),
        in_specs=[ANY, ANY, VM, VM], out_specs=[ANY, ANY],
        scratch_shapes=[
            pltpu.VMEM((NT, D, TB), bf16), pltpu.VMEM((NT, D, TB), bf16),
            pltpu.VMEM((2, 3, FB, TB), f32), pltpu.VMEM((2, 2 * FB, TB), bf16),
            pltpu.VMEM((2, FB, TB), bf16), pltpu.VMEM((NT, D, TB), f32),
            pltpu.VMEM((2, D, TB), bf16),
            pltpu.SemaphoreType.DMA((NT,)), pltpu.SemaphoreType.DMA((NT,)),
            pltpu.SemaphoreType.DMA((2, 3)), pltpu.SemaphoreType.DMA((2,))],
        compiler_params=pltpu.CompilerParams(vmem_limit_bytes=63 << 20),
        cost_estimate=pl.CostEstimate(flops=70_000_000_000, bytes_accessed=60_000_000,
                                      transcendentals=0),
        name="fwd_dx")(x, dy, w, wd)


def kernel_b(x_ref, dy_ref, r_ref, o_ref):
    m = pl.program_id(0)

    @pl.when(m < 2)
    def _():
        o_ref[0] = lax.dot_general(x_ref[...], r_ref[0], NTD, preferred_element_type=f32)

    @pl.when(m == 2)
    def _():
        o_ref[0] = lax.dot_general(dy_ref[...], r_ref[0], NTD, preferred_element_type=f32)


def call_b(x, dy, r):
    bn = 512
    whole = pl.BlockSpec((D, T), lambda m, n: (0, 0), pipeline_mode=pl.Buffered(1))
    return pl.pallas_call(
        kernel_b,
        out_shape=jax.ShapeDtypeStruct((3, D, F), f32), grid=(3, F // bn),
        in_specs=[whole, whole, pl.BlockSpec((1, bn, T), lambda m, n: (m, n, 0))],
        out_specs=pl.BlockSpec((1, D, bn), lambda m, n: (m, 0, n)),
        compiler_params=pltpu.CompilerParams(vmem_limit_bytes=60 << 20),
        cost_estimate=pl.CostEstimate(flops=30_000_000_000, bytes_accessed=60_000_000,
                                      transcendentals=0),
        name="wgrad")(x, dy, r)


def solution(mesh):
    grp = ("fo", "fi")
    alla = ("dp", "fo", "fi")

    def local(x, dy, w1s, w3s, w2s, g):
        wt = jnp.stack([w1s.T, w3s.T, w2s])
        w = lax.all_gather(wt, grp, axis=1, tiled=True)
        w, g = lax.optimization_barrier((w, g))
        gs = lax.psum_scatter(g[0].astype(bf16), grp, scatter_dimension=2, tiled=True)
        wd = w[:2].reshape(2, NF, FB, D).transpose(1, 3, 0, 2).reshape(NF, D, 2 * FB)
        dx, r = call_a(x.T, dy.T, w, wd)
        gs, r = lax.optimization_barrier((gs, r))
        other = lax.ppermute(gs, "dp", [(0, 1), (1, 0)])
        dwl = call_b(x.T, dy.T, r)
        dwn = gs.astype(f32) + other.astype(f32)
        return dx.T, dwn, dwl[None]

    return jax.shard_map(
        local, mesh=mesh,
        in_specs=(P(alla, None), P(alla, None), P(None, grp), P(None, grp), P(grp, None),
                  P(alla, None, None, None)),
        out_specs=(P(alla, None), P(None, None, grp), P(alla, None, None, None)),
        check_vma=False)
```

time: 234 us -> 183 us (0.78)
  matrix products: 138 us -> 0 us
  Pallas kernels: 0 us -> 92.1 us
  blocking collectives: 40.4 us -> 0 us
  waiting for transfers between devices: 25.4 us -> 43.6 us
  local copies, waits for them, and re-layouts: 10.5 us -> 27.5 us
    dot_general x8 -> x0, matrix products: 138 us -> none  [the longest x1 34.2 us: mlp_grads(): dh = jnp.dot(dy, w2t, preferred_element_type=jnp.float32)]
    pallas_call x0 -> x2, Pallas kernels: none -> 92.1 us  [the longest x1 62.2 us: call_a(): pl.pallas_call(kernel_a, out_shape=(jax.ShapeDtypeStruct((D, T), bf16), j...]
    psum x1 -> x0, blocking collectives: 40.4 us -> none  [local(): dwn = lax.psum(gs.astype(jnp.float32), 'dp')]
    all_gather x3 -> x1, waiting for transfers between devices: 23.3 us -> 43.5 us  [local(): w = lax.all_gather(wt, grp, axis=1, tiled=True)]
    reshape x0 -> x2, local copies, waits for them, and re-layouts: none -> 12.7 us  [local(): w[:2].reshape(2, NF, FB, D).transpose(1, 3, 0, 2).reshape(NF, D, 2 * FB)]
    unnamed x5 -> x2, local copies, waits for them, and re-layouts: 10.5 us -> 0.01 us
    optimization_barrier x0 -> x1, local copies, waits for them, and re-layouts: none -> 10.4 us  [local(): w, g = lax.optimization_barrier((w, g))]
    broadcast_in_dim x1 -> x0, other arithmetic: 5.13 us -> none  [local(): return (dx, dwn, dwl[None])]
  transfers between devices with their start and end apart: 4 -> 3, of which waited for: 2 -> 1; matrix products, arithmetic and copies ran while one was open for 66% -> 9% of each run, Pallas kernels for 0% -> 51%
where the time goes in v1:
time: 183 us; the launch traced here: 182 us
  Pallas kernels  92.1 us (50%)
  waiting for transfers between devices  43.6 us (24%)
  local copies, waits for them, and re-layouts  27.5 us (15%)
  between operations  14.1 us (8%)
  other arithmetic  3.43 us (2%)
    pallas_call x1, Pallas kernels, call_a(): pl.pallas_call(kernel_a, out_shape=(jax.ShapeDtypeStruct((D, T), bf16), j...  62.2 us
    all_gather x1, waiting for transfers between devices, local(): w = lax.all_gather(wt, grp, axis=1, tiled=True)  43.5 us
    pallas_call x1, Pallas kernels, call_b(): pl.pallas_call(kernel_b, out_shape=jax.ShapeDtypeStruct((3, D, F), f32),...  29.9 us
    reshape x2, local copies, waits for them, and re-layouts, local(): w[:2].reshape(2, NF, FB, D).transpose(1, 3, 0, 2).reshape(NF, D, 2 * FB)  12.7 us
    optimization_barrier x1, local copies, waits for them, and re-layouts, local(): w, g = lax.optimization_barrier((w, g))  10.4 us
    slice x1, local copies, waits for them, and re-layouts, local(): w[:2].reshape(2, NF, FB, D).transpose(1, 3, 0, 2).reshape(NF, D, 2 * FB)  4.37 us
  transfers between devices with their start and end apart: 3, of which 1 were waited for; matrix products, arithmetic and copies ran while one was open for 9% of the time, Pallas kernels for 51%

profile of v1, /device:TPU:0, one launch (start us, length us, event | category | flops | bytes accessed | tf_op | source)
XLA Modules:
  0.0 182.3 jit_solution(5249944485879051757)
XLA Ops:
  7.2 0.0 all-gather.2.cloned.1.call-start
  7.2 2.2 %pad_maximum_fusion = bf16[3,192,576]{2,1,0:T(8,128)(2,1)} fusion(bf16[1,192,576]{2,1,0:T(8,128)(2,1)} %bitcast.19, bf16[1,192,576]{2,1,0:T(8,128)(2,1)} %bitcast.20, bf16[1,192,576]{2,1,0:T(8,128)(2,1)} %bitcast.21), kind=kLoop, calls=%fused_computation.2 | loop fusion | flops 663552 | bytes 1327104 | tf_op jit(solution)/shard_map/stack | solution.py:164
  9.4 0.0 all-gather.2.cloned.1.call-update
  9.4 0.0 reduce-scatter.2.cloned.1.call-start
  9.5 43.5 %all-gather.2.cloned.1.call-done.w_ref = bf16[3,1536,576]{2,1,0:T(8,128)(2,1)} async-done(((bf16[3,192,576]{2,1,0:T(8,128)(2,1)}), bf16[3,1536,576]{2,1,0:T(8,128)(2,1)}) %all-gather.2.cloned.1.call-update) | async-done | bytes 5308432 | tf_op jit(solution)/shard_map/all_gather | solution.py:165
  53.0 10.4 %copy.10 = bf16[1,3,576,1536]{2,3,1,0:T(8,128)(2,1)} copy(f32[1,3,576,1536]{3,2,1,0:T(8,128)} %param.11) | data formatting | bytes 15925248 | tf_op jit(solution)/shard_map/optimization_barrier | solution.py:166
  63.4 0.0 reduce-scatter.2.cloned.1.call-update
  63.4 4.4 %slice.3 = bf16[2,1536,576]{2,1,0:T(8,128)(2,1)} slice(bf16[3,1536,576]{2,1,0:T(8,128)(2,1)} %all-gather.2.cloned.1.call-done.w_ref), slice={[0:2], [0:1536], [0:576]} | slice | bytes 7077888 | tf_op jit(solution)/shard_map/slice | solution.py:168
  67.8 8.7 %copy.9 = bf16[2,4,384,576]{2,0,3,1:T(2,128)(2,1)S(1)} copy(bf16[2,4,384,576]{3,2,1,0:T(8,128)(2,1)} %bitcast.17) | data formatting | bytes 7077888 | tf_op jit(solution)/shard_map/reshape | solution.py:168
  76.5 4.0 %reshape.14.wd_ref = bf16[4,576,768]{2,1,0:T(8,128)(2,1)} reshape(bf16[4,576,2,384]{3,2,1,0:T(2,128)(2,1)S(1)} %bitcast.18) | data formatting | bytes 7077888 | tf_op jit(solution)/shard_map/reshape | solution.py:168
  80.5 62.2 %fwd_dx.1 = (bf16[576,4096]{1,0:T(8,128)(2,1)}, bf16[3,1536,4096]{2,1,0:T(8,128)(2,1)}) custom-call(bf16[576,4096]{1,0:T(8,128)(2,1)} %bitcast.22, bf16[576,4096]{1,0:T(8,128)(2,1)} %bitcast.24, bf16[3,1536,576]{2,1,0:T(8,128)(2,1)} %all-gather.2.cloned.1.call-done.w_ref, bf16[4,576,768]{2,1,0:T(8,128)(2,1)} %reshape.14.wd_ref), custom_call_target="tpu_custom_call" | custom-call | flops 70000001024 | bytes 60000000 | tf_op jit(solution)/shard_map/fwd_dx/pallas_call | solution.py:116
  142.7 0.0 reduce-scatter.2.cloned.1.call-done
  142.7 0.0 copy-start
  142.7 1.5 collective-permute-start
  144.2 29.9 %wgrad.1 = f32[3,576,1536]{2,1,0:T(8,128)} custom-call(bf16[576,4096]{1,0:T(8,128)(2,1)} %bitcast.23, bf16[576,4096]{1,0:T(8,128)(2,1)} %bitcast.25, bf16[3,1536,4096]{2,1,0:T(8,128)(2,1)} %get-tuple-element.14.r_ref), custom_call_target="tpu_custom_call" | custom-call | flops 30000001024 | bytes 60000000 | tf_op jit(solution)/shard_map/wgrad/pallas_call | solution.py:148
  174.2 0.0 collective-permute-done
  174.2 0.0 copy-done
  174.2 1.3 convert_add_fusion
Async XLA Ops:
  7.2 45.8 %all-gather.2.cloned.1.call-start = ((), (), s32[]{:S(2)}) async-start(), calls=%async_computation.1 | async-start | bytes 6635520 | tf_op jit(solution)/shard_map/all_gather | solution.py:165
  9.4 133.3 %reduce-scatter.2.cloned.1.call-start = ((), (), s32[]{:S(2)}) async-start(), calls=%async_computation.2 | async-start | bytes 6635520 | tf_op jit(solution)/shard_map/reduce_scatter | solution.py:167
  142.7 31.5 %copy-start = (bf16[3,576,192]{1,2,0:T(8,128)(2,1)S(1)}, bf16[3,576,192]{1,2,0:T(8,128)(2,1)}, u32[]{:S(2)}) copy-start(bf16[3,576,192]{1,2,0:T(8,128)(2,1)} %reduce-scatter.2.cloned.1.call-done) | copy-start | bytes 1990660
  142.7 31.4 %collective-permute-start = (bf16[3,576,192]{1,2,0:T(8,128)(2,1)}, bf16[3,576,192]{1,2,0:T(8,128)(2,1)S(1)}, u32[]{:S(2)}, u32[]{:S(2)}) collective-permute-start(bf16[3,576,192]{1,2,0:T(8,128)(2,1)} %reduce-scatter.2.cloned.1.call-done), channel_id=1, source_target_pairs={{0,8},{8,0},{1,9},{9,1},{2,10},{10,2},{3,11},{11,3},{4,12},{12,4},... | collective-permute-start | bytes 1990664 | tf_op jit(solution)/shard_map/ppermute | solution.py:171
Sparse Core Ops, SparseCore 0:
  10.4 42.5 all-gather.1
  63.6 53.3 reduce-scatter.1

commit v2 on v1

v2 whole, which is shorter than its diff:
```python
import jax
import jax.numpy as jnp
from jax import lax
from jax.experimental import pallas as pl
from jax.experimental.pallas import tpu as pltpu
from jax.sharding import PartitionSpec as P

bf16, f32 = jnp.bfloat16, jnp.float32
T, D, F = 4096, 576, 1536
FB, TB, RC = 384, 512, 16
NF, NT = F // FB, T // TB
NN = (((1,), (0,)), ((), ()))
NTD = (((1,), (1,)), ((), ()))
ANY = pl.BlockSpec(memory_space=pl.ANY)
VM = pl.BlockSpec(memory_space=pltpu.VMEM)


def dot(a, b):
    return lax.dot_general(a, b, NN, preferred_element_type=f32)


def kernel_a(x_hbm, dy_hbm, w1_hbm, w3_hbm, w2_hbm, g_hbm, dx_hbm, r_hbm, z_hbm,
             x, dy, acts, dd, hh, dxa, dxo, wg, wd, gst, sb, rb, r0, r1, r2, qb, fin, rz, zf, zr,
             sx, sd, so, sdx, sw, sg, ssem, rsem):
    zi, yi, fi = lax.axis_index("dp"), lax.axis_index("fo"), lax.axis_index("fi")
    xi, ci = fi // 2, fi % 2
    to_c = (zi, yi, xi * 2 + 1 - ci)
    to_x = (zi, yi, (1 - xi) * 2 + ci)
    to_y = (zi, 1 - yi, fi)
    to_z = (1 - zi, yi, fi)
    own = ci * 192
    half, other = own + zi * 96, own + (1 - zi) * 96

    def blk(yy, xx):
        return pl.ds(pl.multiple_of((yy * 2 + xx) * FB, FB), FB)

    def wrows(j, r, n):
        return wg.at[j, :, pl.ds(pl.multiple_of(r, 16), n), :]

    def piece(k, yy, xx):
        return rb.at[pl.ds(2 * k, 2), :, blk(yy, xx)]

    table = [
        (wrows(0, own, 192), wrows(0, own, 192), to_c),
        (wrows(0, own, 192), wrows(1, own, 192), to_x),
        (wrows(0, half, 96), wrows(2, half, 96), to_y),
        (wrows(1, own, 192), wrows(1, own, 192), to_c),
        (wrows(2, half, 96), wrows(2, half, 96), to_z),
        (wrows(2, half, 96), wrows(2, half, 96), to_c),
        (wrows(2, other, 96), wrows(2, other, 96), to_c),
        (wrows(1, half, 48), wrows(3, half, 48), to_y),
        (wrows(2, half + 48, 48), wrows(3, half + 48, 48), to_x),
        (wrows(3, half, 96), wrows(3, half, 96), to_z),
        (wrows(3, half, 96), wrows(3, half, 96), to_c),
        (wrows(3, other, 96), wrows(3, other, 96), to_c),
        (sb.at[pl.ds(0, 3)], rb.at[pl.ds(0, 3)], to_c),
        (sb.at[pl.ds(3, 3)], rb.at[pl.ds(3, 3)], to_c),
        (piece(0, 1 - yi, 1 - xi), r0.at[0], to_y),
        (piece(1, 1 - yi, 1 - xi), r0.at[1], to_y),
        (piece(2, 1 - yi, 1 - xi), r0.at[2], to_x),
        (piece(0, 1 - yi, xi), r1.at[0], to_y),
        (piece(1, 1 - yi, xi), r1.at[1], to_y),
        (piece(2, yi, 1 - xi), r1.at[2], to_x),
        (qb.at[0], r2.at[0], to_x),
        (qb.at[1], r2.at[1], to_x),
        (qb.at[2], r2.at[2], to_y),
        (fin.at[0], rz.at[0], to_z),
        (fin.at[1], rz.at[1], to_z),
        (fin.at[2], rz.at[2], to_z),
        (zf.at[pl.ds(0, 4)], zr.at[pl.ds(0, 4)], to_c),
        (zf.at[pl.ds(4, 2)], zr.at[pl.ds(4, 2)], to_c),
    ]

    def rc(k):
        src, dst, dev = table[k]
        return pltpu.make_async_remote_copy(src, dst, ssem.at[k], rsem.at[k], device_id=dev,
                                            device_id_type=pl.DeviceIdType.MESH)

    def start(*ks):
        for k in ks:
            rc(k).start()

    def arrived(*ks):
        for k in ks:
            rc(k).wait_recv()

    def xcp(t):
        return pltpu.make_async_copy(x_hbm.at[:, pl.ds(t * TB, TB)], x.at[t], sx.at[t])

    def dcp(t):
        return pltpu.make_async_copy(dy_hbm.at[:, pl.ds(t * TB, TB)], dy.at[t], sd.at[t])

    def gcp(i, side):
        return pltpu.make_async_copy(g_hbm.at[pl.ds(side * 6 + i * 3, 3)], gst.at[i], sg.at[i])

    wcps = [pltpu.make_async_copy(h, wg.at[0, m, pl.ds(pl.multiple_of(own, 192), 192), :], sw.at[m])
            for m, h in enumerate((w1_hbm, w3_hbm, w2_hbm))]
    for cp in wcps:
        cp.start()
    bar = pltpu.get_barrier_semaphore()
    for dev in (to_c, to_x, to_y, to_z):
        pl.semaphore_signal(bar, inc=1, device_id=dev, device_id_type=pl.DeviceIdType.MESH)
    xcp(0).start()
    dcp(0).start()
    xcp(1).start()
    dcp(1).start()
    for i in (0, 1):
        gcp(i, 1 - ci).start()
    for t in range(2, NT):
        xcp(t).start()
        dcp(t).start()
    dd[1] = jnp.zeros(dd.shape[1:], bf16)
    for cp in wcps:
        cp.wait()
    pl.semaphore_wait(bar, 4)
    start(0, 1, 2)

    def flip(j):
        for m in (0, 1):
            wd[j, :, m * FB:(m + 1) * FB] = wg[j, m].T

    def outcp(s, p):
        j = s // NT
        yj = yi + (j // 2) * (1 - 2 * yi)
        xj = xi + (j % 2) * (1 - 2 * xi)
        ts = pl.ds(pl.multiple_of(s % NT * TB, TB), TB)
        fs = pl.ds(pl.multiple_of((yj * 2 + xj) * FB, FB), FB)
        return [pltpu.make_async_copy(dd.at[p, pl.ds(0, FB)], r_hbm.at[0, fs, ts], so.at[p, 0]),
                pltpu.make_async_copy(dd.at[p, pl.ds(FB, FB)], r_hbm.at[1, fs, ts], so.at[p, 1]),
                pltpu.make_async_copy(hh.at[p], r_hbm.at[2, fs, ts], so.at[p, 2])]

    def fwd(f, t, p):
        acts[p, 0] = dot(wg[f, 0], x[t])
        acts[p, 1] = dot(wg[f, 1], x[t])
        acts[p, 2] = dot(wg[f, 2], dy[t])

    def ew(p):
        for r in range(0, FB, RC):
            a, b, dh = (acts[p, k, r:r + RC, :] for k in range(3))
            s = 0.5 * jnp.tanh(0.5 * a) + 0.5
            sa = a * s
            hh[p, r:r + RC, :] = (sa * b).astype(bf16)
            dd[p, r:r + RC, :] = (dh * b * (s * (1.0 + a * (1.0 - s)))).astype(bf16)
            dd[p, FB + r:FB + r + RC, :] = (dh * sa).astype(bf16)

    def dxp(s, p, first):
        t = s % NT
        if first:
            dxa[t] = dot(wd[0], dd[p])
        else:
            dxa[t] += dot(wd[s // NT], dd[p])

    def tiles(i, first, extra=None):
        s0 = 2 * i
        f, t0 = s0 // NT, s0 % NT

        def drain(p):
            for cp in outcp(s0 - 2 + p, p):
                cp.wait()

        if first:
            @pl.when(i > 0)
            def _():
                drain(0)
        else:
            drain(0)
        fwd(f, t0, 0)
        ew(0)
        if extra is not None:
            extra(0)
        dxp(s0 + NT - 1 if first else s0 - 1, 1, first)
        if first:
            @pl.when(i > 0)
            def _():
                drain(1)
        else:
            drain(1)
        for cp in outcp(s0, 0):
            cp.start()
        fwd(f, t0 + 1, 1)
        ew(1)
        if extra is not None:
            extra(1)
        dxp(s0, 0, first)
        for cp in outcp(s0 + 1, 1):
            cp.start()

    def need(i):
        for t in (2 * i, 2 * i + 1):
            xcp(t).wait()
            dcp(t).wait()

    def phase0a(i, c):
        need(i)
        gcp(i, 1 - ci).wait()

        def conv(h):
            for gr in range(3):
                for r in range(72 * h, 72 * h + 72, 24):
                    sb[i * 3 + gr, r:r + 24, :] = gst[i, gr, r:r + 24, :].astype(bf16)

        tiles(i, True, conv)

        @pl.when(i == 0)
        def _():
            start(12)

        @pl.when(i == 1)
        def _():
            start(13)

        gcp(i, ci).start()
        return c

    def phase0b(i, c):
        need(i + 2)
        gcp(i, ci).wait()

        @pl.when(i == 0)
        def _():
            arrived(12)

        @pl.when(i == 1)
        def _():
            arrived(13)
            start(14)
            arrived(2)
            start(4, 5, 8)

        def conv(h):
            for gr in range(3):
                for r in range(72 * h, 72 * h + 72, 24):
                    v = gst[i, gr, r:r + 24, :].astype(bf16).astype(f32)
                    v = v + rb[i * 3 + gr, r:r + 24, :].astype(f32)
                    rb[i * 3 + gr, r:r + 24, :] = v.astype(bf16)

        tiles(i + 2, True, conv)
        return c

    arrived(0)
    flip(0)
    lax.fori_loop(0, 2, phase0a, 0)
    lax.fori_loop(0, 2, phase0b, 0)
    start(15, 16)
    arrived(1)
    start(3, 7)
    arrived(3)
    flip(1)
    start(17, 18)

    def relay(k, yy, xx):
        qb[k] = (rb[2 * k:2 * k + 2, :, blk(yy, xx)].astype(f32) + r0[k].astype(f32)).astype(bf16)

    def group_sum(k):
        fin[k] = (rb[2 * k:2 * k + 2, :, blk(yi, xi)].astype(f32) + r1[k].astype(f32)
                  + r2[k].astype(f32)).astype(bf16)

    def total(k):
        zf[2 * k:2 * k + 2] = fin[k].astype(f32) + rz[k].astype(f32)

    def at5():
        arrived(14)
        relay(0, yi, 1 - xi)
        start(20)
        arrived(4)
        start(6)

    def at6():
        arrived(15)
        relay(1, yi, 1 - xi)
        start(21)

    def at7():
        arrived(7, 8)
        start(9, 10)
        arrived(16)
        relay(2, 1 - yi, xi)
        start(22, 19)

    def at8():
        arrived(5, 6)
        flip(2)

    def at10():
        arrived(17, 20)
        group_sum(0)
        start(23)

    def at11():
        arrived(18, 21)
        group_sum(1)
        start(24)
        arrived(9)
        start(11)

    def at12():
        arrived(10, 11)
        flip(3)
        arrived(19, 22)
        group_sum(2)
        start(25)

    def at15():
        arrived(23, 24)
        total(0)
        total(1)
        start(26)

    events = {5: at5, 6: at6, 7: at7, 8: at8, 10: at10, 11: at11, 12: at12, 15: at15}

    def phase1(i, c):
        for k, ev in events.items():
            pl.when(i == k)(ev)
        tiles(i, False)
        return c

    n = NF * NT
    lax.fori_loop(NT // 2, n // 2, phase1, 0)
    arrived(25)
    total(2)
    start(27)
    dxp(n - 1, 1, False)

    def ocp(t, p):
        return pltpu.make_async_copy(dxo.at[p], dx_hbm.at[:, pl.ds(t * TB, TB)], sdx.at[p])

    for t in range(NT):
        p = t % 2
        if t >= 2:
            ocp(t - 2, p).wait()
        dxo[p] = dxa[t].astype(bf16)
        ocp(t, p).start()
    zown = pltpu.make_async_copy(zf, z_hbm.at[pl.ds(ci * 6, 6)], sg.at[0])
    zoth = pltpu.make_async_copy(zr, z_hbm.at[pl.ds(6 - ci * 6, 6)], sg.at[1])
    zown.start()
    arrived(26, 27)
    zoth.start()
    for p in (0, 1):
        for cp in outcp(n - 2 + p, p):
            cp.wait()
    ocp(NT - 2, 0).wait()
    ocp(NT - 1, 1).wait()
    for k in range(len(table)):
        rc(k).wait_send()
    zown.wait()
    zoth.wait()


def call_a(x, dy, w1, w3, w2, g):
    part = (3, 2, 144, FB)
    return pl.pallas_call(
        kernel_a,
        out_shape=(jax.ShapeDtypeStruct((D, T), bf16), jax.ShapeDtypeStruct((3, F, T), bf16),
                   jax.ShapeDtypeStruct((12, 144, FB), f32)),
        in_specs=[ANY] * 6, out_specs=[ANY] * 3,
        scratch_shapes=[
            pltpu.VMEM((NT, D, TB), bf16), pltpu.VMEM((NT, D, TB), bf16),
            pltpu.VMEM((2, 3, FB, TB), f32), pltpu.VMEM((2, 2 * FB, TB), bf16),
            pltpu.VMEM((2, FB, TB), bf16), pltpu.VMEM((NT, D, TB), f32),
            pltpu.VMEM((2, D, TB), bf16),
            pltpu.VMEM((NF, 3, FB, D), bf16), pltpu.VMEM((NF, D, 2 * FB), bf16),
            pltpu.VMEM((2, 3, 144, F), f32), pltpu.VMEM((6, 144, F), bf16),
            pltpu.VMEM((6, 144, F), bf16),
            pltpu.VMEM(part, bf16), pltpu.VMEM(part, bf16), pltpu.VMEM(part, bf16),
            pltpu.VMEM(part, bf16), pltpu.VMEM(part, bf16), pltpu.VMEM(part, bf16),
            pltpu.VMEM((6, 144, FB), f32), pltpu.VMEM((6, 144, FB), f32),
            pltpu.SemaphoreType.DMA((NT,)), pltpu.SemaphoreType.DMA((NT,)),
            pltpu.SemaphoreType.DMA((2, 3)), pltpu.SemaphoreType.DMA((2,)),
            pltpu.SemaphoreType.DMA((3,)), pltpu.SemaphoreType.DMA((2,)),
            pltpu.SemaphoreType.DMA((28,)), pltpu.SemaphoreType.DMA((28,))],
        compiler_params=pltpu.CompilerParams(vmem_limit_bytes=67043328, collective_id=0,
                                             has_side_effects=True),
        cost_estimate=pl.CostEstimate(flops=40_000_000_000, bytes_accessed=60_000_000,
                                      transcendentals=0),
        name="fwd_dx")(x, dy, w1, w3, w2, g)


def kernel_b(x_ref, dy_ref, r_ref, o_ref):
    m = pl.program_id(0)

    @pl.when(m < 2)
    def _():
        o_ref[0] = lax.dot_general(x_ref[...], r_ref[0], NTD, preferred_element_type=f32)

    @pl.when(m == 2)
    def _():
        o_ref[0] = lax.dot_general(dy_ref[...], r_ref[0], NTD, preferred_element_type=f32)


def call_b(x, dy, r):
    bn = 512
    whole = pl.BlockSpec((D, T), lambda m, n: (0, 0), pipeline_mode=pl.Buffered(1))
    return pl.pallas_call(
        kernel_b,
        out_shape=jax.ShapeDtypeStruct((3, D, F), f32), grid=(3, F // bn),
        in_specs=[whole, whole, pl.BlockSpec((1, bn, T), lambda m, n: (m, n, 0))],
        out_specs=pl.BlockSpec((1, D, bn), lambda m, n: (m, 0, n)),
        compiler_params=pltpu.CompilerParams(vmem_limit_bytes=60 << 20),
        cost_estimate=pl.CostEstimate(flops=30_000_000_000, bytes_accessed=60_000_000,
                                      transcendentals=0),
        name="wgrad")(x, dy, r)


def solution(mesh):
    grp = ("fo", "fi")
    alla = ("dp", "fo", "fi")

    def local(x, dy, w1s, w3s, w2s, g):
        dx, r, z = call_a(x.T, dy.T, w1s.T, w3s.T, w2s, g.reshape(12, 144, F))
        dwl = call_b(x.T, dy.T, r)
        dwn = lax.dynamic_slice_in_dim(z.reshape(3, D, FB), lax.axis_index("fi") % 2 * 192, 192, 2)
        return dx.T, dwn, dwl[None]

    return jax.shard_map(
        local, mesh=mesh,
        in_specs=(P(alla, None), P(alla, None), P(None, grp), P(None, grp), P(grp, None),
                  P(alla, None, None, None)),
        out_specs=(P(alla, None), P(None, None, grp), P(alla, None, None, None)),
        check_vma=False)
```

time: 183 us -> 110 us (0.60)
  waiting for transfers between devices: 43.6 us -> 0 us
  local copies, waits for them, and re-layouts: 27.5 us -> 9.1 us
  between operations: 14.1 us -> 0.66 us
  Pallas kernels: 92.1 us -> 99.9 us
  other arithmetic: 3.43 us -> 0 us
    all_gather x1 -> x0, waiting for transfers between devices: 43.5 us -> none  [local(): w = lax.all_gather(wt, grp, axis=1, tiled=True)]
    reshape x2 -> x0, local copies, waits for them, and re-layouts: 12.7 us -> none  [local(): w[:2].reshape(2, NF, FB, D).transpose(1, 3, 0, 2).reshape(NF, D, 2 * FB)]
    optimization_barrier x1 -> x0, local copies, waits for them, and re-layouts: 10.4 us -> none  [local(): w, g = lax.optimization_barrier((w, g))]
    pallas_call x1, Pallas kernels: 62.2 us -> 70 us  [call_a(): pl.pallas_call(kernel_a, out_shape=(jax.ShapeDtypeStruct((D, T), bf16), j...]
    unnamed x2, local copies, waits for them, and re-layouts: 0.01 us -> 6.82 us
    slice x1 -> x0, local copies, waits for them, and re-layouts: 4.37 us -> none  [local(): w[:2].reshape(2, NF, FB, D).transpose(1, 3, 0, 2).reshape(NF, D, 2 * FB)]
    dynamic_slice x0 -> x1, local copies, waits for them, and re-layouts: none -> 2.28 us  [local(): lax.dynamic_slice_in_dim(z.reshape(3, D, FB), lax.axis_index('fi') % 2 *...]
    another operation x1 -> x0, other arithmetic: 2.17 us -> none  [local(): wt = jnp.stack([w1s.T, w3s.T, w2s])]
  transfers between devices with their start and end apart: 3 -> 0, of which waited for: 1 -> 0; matrix products, arithmetic and copies ran while one was open for 9% -> 0% of each run, Pallas kernels for 51% -> 0%
where the time goes in v2:
time: 110 us
  Pallas kernels  99.9 us (91%)
  local copies, waits for them, and re-layouts  9.1 us (8%)
    pallas_call x1, Pallas kernels, call_a(): pl.pallas_call(kernel_a, out_shape=(jax.ShapeDtypeStruct((D, T), bf16), j...  70 us
    pallas_call x1, Pallas kernels, call_b(): pl.pallas_call(kernel_b, out_shape=jax.ShapeDtypeStruct((3, D, F), f32),...  29.9 us
    unnamed x2, local copies, waits for them, and re-layouts  6.82 us
    dynamic_slice x1, local copies, waits for them, and re-layouts, local(): lax.dynamic_slice_in_dim(z.reshape(3, D, FB), lax.axis_index('fi') % 2 *...  2.28 us

profile of v2, /device:TPU:0, one launch (start us, length us, event | category | flops | bytes accessed | tf_op | source)
XLA Modules:
  0.0 109.6 jit_solution(2783019302810700973)
XLA Ops:
  0.6 70.0 %fwd_dx.1 = (bf16[576,4096]{1,0:T(8,128)(2,1)}, bf16[3,1536,4096]{2,1,0:T(8,128)(2,1)}, f32[12,144,384]{2,1,0:T(8,128)}) custom-call(bf16[576,4096]{1,0:T(8,128)(2,1)} %bitcast.11, bf16[576,4096]{1,0:T(8,128)(2,1)} %bitcast.13, bf16[192,576]{1,0:T(8,128)(2,1)} %bitcast.15, bf16[192,576]{1,0:T(8,128)(2,1)} %bitcast.16, bf16[192,576]{1,0:T(8,128)(2,1)} %w2_hbm.1, ...), custom_call_target="tpu_custom_call" | custom-call | flops 40000000000 | bytes 60000000 | tf_op jit(solution)/shard_map/fwd_dx/pallas_call | solution.py:351
  70.6 2.3 %constant_dynamic-slice_fusion = f32[3,576,192]{2,1,0:T(8,128)S(1)} fusion(f32[3,576,384]{2,1,0:T(8,128)} %bitcast.9, s32[]{:T(128)S(6)} %select_n.11), kind=kLoop, calls=%fused_computation | loop fusion | bytes 2654212 | tf_op jit(solution)/shard_map/dynamic_slice | solution.py:411
  72.9 1.7 %copy.10 = f32[3,576,192]{1,2,0:T(8,128)} copy(f32[3,576,192]{2,1,0:T(8,128)S(1)} %constant_dynamic-slice_fusion) | data formatting | bytes 2654208
  74.6 29.9 %wgrad.1 = f32[3,576,1536]{2,1,0:T(8,128)} custom-call(bf16[576,4096]{1,0:T(8,128)(2,1)} %bitcast.12, bf16[576,4096]{1,0:T(8,128)(2,1)} %bitcast.14, bf16[3,1536,4096]{2,1,0:T(8,128)(2,1)} %get-tuple-element.8.r_ref), custom_call_target="tpu_custom_call" | custom-call | flops 30000001024 | bytes 60000000 | tf_op jit(solution)/shard_map/wgrad/pallas_call | solution.py:393
  104.5 5.1 %copy.12 = bf16[4096,576]{0,1:T(8,128)(2,1)} copy(bf16[4096,576]{0,1:T(8,128)(2,1)} %bitcast.8) | data formatting | bytes 9437184

commit v3 on v2

--- a/solution.py
+++ b/solution.py
@@ -20,8 +20,10 @@
 
 
 def kernel_a(x_hbm, dy_hbm, w1_hbm, w3_hbm, w2_hbm, g_hbm, dx_hbm, r_hbm, z_hbm,
-             x, dy, acts, dd, hh, dxa, dxo, wg, wd, gst, sb, rb, r0, r1, r2, qb, fin, rz, zf, zr,
+             x, dy, acts, dda, ddb, hha, hhb, dxa, dxoa, dxob, wg, wd, gst, sb, rb, r0, r1, r2,
+             qb, fin, rz, zf, zr,
              sx, sd, so, sdx, sw, sg, ssem, rsem):
+    dd, hh, dxo = (dda, ddb), (hha, hhb), (dxoa, dxob)
     zi, yi, fi = lax.axis_index("dp"), lax.axis_index("fo"), lax.axis_index("fi")
     xi, ci = fi // 2, fi % 2
     to_c = (zi, yi, xi * 2 + 1 - ci)
@@ -109,7 +111,7 @@
     for t in range(2, NT):
         xcp(t).start()
         dcp(t).start()
-    dd[1] = jnp.zeros(dd.shape[1:], bf16)
+    ddb[1] = jnp.zeros(ddb.shape[1:], bf16)
     for cp in wcps:
         cp.wait()
     pl.semaphore_wait(bar, 4)
@@ -119,71 +121,80 @@
         for m in (0, 1):
             wd[j, :, m * FB:(m + 1) * FB] = wg[j, m].T
 
-    def outcp(s, p):
-        j = s // NT
+    def outs(s0, q):
+        j = s0 // NT
         yj = yi + (j // 2) * (1 - 2 * yi)
         xj = xi + (j % 2) * (1 - 2 * xi)
-        ts = pl.ds(pl.multiple_of(s % NT * TB, TB), TB)
-        fs = pl.ds(pl.multiple_of((yj * 2 + xj) * FB, FB), FB)
-        return [pltpu.make_async_copy(dd.at[p, pl.ds(0, FB)], r_hbm.at[0, fs, ts], so.at[p, 0]),
-                pltpu.make_async_copy(dd.at[p, pl.ds(FB, FB)], r_hbm.at[1, fs, ts], so.at[p, 1]),
-                pltpu.make_async_copy(hh.at[p], r_hbm.at[2, fs, ts], so.at[p, 2])]
+        fs = blk(yj, xj)
+        res = []
+        for p in (0, 1):
+            ts = pl.ds(pl.multiple_of((s0 + p) % NT * TB, TB), TB)
+            for m, src in enumerate((dd[p].at[q, pl.ds(0, FB)], dd[p].at[q, pl.ds(FB, FB)], hh[p].at[q])):
+                res.append(pltpu.make_async_copy(src, r_hbm.at[m, fs, ts], so.at[q, p, m]))
+        return res
 
     def fwd(f, t, p):
         acts[p, 0] = dot(wg[f, 0], x[t])
         acts[p, 1] = dot(wg[f, 1], x[t])
         acts[p, 2] = dot(wg[f, 2], dy[t])
 
-    def ew(p):
+    def ew(p, q):
         for r in range(0, FB, RC):
             a, b, dh = (acts[p, k, r:r + RC, :] for k in range(3))
             s = 0.5 * jnp.tanh(0.5 * a) + 0.5
             sa = a * s
-            hh[p, r:r + RC, :] = (sa * b).astype(bf16)
-            dd[p, r:r + RC, :] = (dh * b * (s * (1.0 + a * (1.0 - s)))).astype(bf16)
-            dd[p, FB + r:FB + r + RC, :] = (dh * sa).astype(bf16)
-
-    def dxp(s, p, first):
+            hh[p][q, r:r + RC, :] = (sa * b).astype(bf16)
+            dd[p][q, r:r + RC, :] = (dh * b * (s * (1.0 + a * (1.0 - s)))).astype(bf16)
+            dd[p][q, FB + r:FB + r + RC, :] = (dh * sa).astype(bf16)
+
+    def ocp(s, q, p):
+        ts = pl.ds(pl.multiple_of(s % NT * TB, TB), TB)
+        return pltpu.make_async_copy(dxo[p].at[q], dx_hbm.at[:, ts], sdx.at[q, p])
+
+    def dxp(s, q, p, first, o=None):
         t = s % NT
         if first:
-            dxa[t] = dot(wd[0], dd[p])
+            dxa[t] = dot(wd[0], dd[p][q])
+            return
+        v = dxa[t] + dot(wd[s // NT], dd[p][q])
+        dxa[t] = v
+        if o is not None:
+            dxo[p][o] = v.astype(bf16)
+
+    def tiles(i, first, extra=None, last=False):
+        s0, q = 2 * i, i % 2
+        f, t0 = s0 // NT, s0 % NT
+
+        def drain():
+            for cp in outs(s0 - 4, q):
+                cp.wait()
+
+        if first:
+            pl.when(i > 1)(drain)
         else:
-            dxa[t] += dot(wd[s // NT], dd[p])
-
-    def tiles(i, first, extra=None):
-        s0 = 2 * i
-        f, t0 = s0 // NT, s0 % NT
-
-        def drain(p):
-            for cp in outcp(s0 - 2 + p, p):
-                cp.wait()
-
-        if first:
-            @pl.when(i > 0)
+            drain()
+        if last:
+            @pl.when(i > 13)
             def _():
-                drain(0)
-        else:
-            drain(0)
+                ocp(s0 - 5, q, 1).wait()
+                ocp(s0 - 4, q, 0).wait()
+
+        o = q if last else None
         fwd(f, t0, 0)
-        ew(0)
+        ew(0, q)
         if extra is not None:
             extra(0)
-        dxp(s0 + NT - 1 if first else s0 - 1, 1, first)
-        if first:
-            @pl.when(i > 0)
-            def _():
-                drain(1)
-        else:
-            drain(1)
-        for cp in outcp(s0, 0):
-            cp.start()
+        dxp(s0 + NT - 1 if first else s0 - 1, 1 - q, 1, first, o)
         fwd(f, t0 + 1, 1)
-        ew(1)
+        ew(1, q)
         if extra is not None:
             extra(1)
-        dxp(s0, 0, first)
-        for cp in outcp(s0 + 1, 1):
+        dxp(s0, q, 0, first, o)
+        for cp in outs(s0, q):
             cp.start()
+        if last:
+            ocp(s0 - 1, q, 1).start()
+            ocp(s0, q, 0).start()
 
     def need(i):
         for t in (2 * i, 2 * i + 1):
@@ -306,7 +317,7 @@
         total(1)
         start(26)
 
-    events = {5: at5, 6: at6, 7: at7, 8: at8, 10: at10, 11: at11, 12: at12, 15: at15}
+    events = {5: at5, 6: at6, 7: at7, 8: at8, 10: at10, 11: at11}
 
     def phase1(i, c):
         for k, ev in events.items():
@@ -314,40 +325,46 @@
         tiles(i, False)
         return c
 
+    def phase2(i, c):
+        pl.when(i == 15)(at15)
+        tiles(i, False, last=True)
+        return c
+
     n = NF * NT
-    lax.fori_loop(NT // 2, n // 2, phase1, 0)
+    lax.fori_loop(NT // 2, 12, phase1, 0)
+    at12()
+    lax.fori_loop(12, n // 2, phase2, 0)
+    ocp(n - 5, 0, 1).wait()
+    dxp(n - 1, 1, 1, False, 0)
+    ocp(n - 1, 0, 1).start()
+    zown = [pltpu.make_async_copy(zf.at[pl.ds(a, k)], z_hbm.at[pl.ds(ci * 6 + a, k)], sg.at[q])
+            for q, (a, k) in enumerate(((0, 4), (4, 2)))]
+    zoth = [pltpu.make_async_copy(zr.at[pl.ds(a, k)], z_hbm.at[pl.ds(6 - ci * 6 + a, k)], sw.at[q])
+            for q, (a, k) in enumerate(((0, 4), (4, 2)))]
+    zown[0].start()
     arrived(25)
     total(2)
     start(27)
-    dxp(n - 1, 1, False)
-
-    def ocp(t, p):
-        return pltpu.make_async_copy(dxo.at[p], dx_hbm.at[:, pl.ds(t * TB, TB)], sdx.at[p])
-
-    for t in range(NT):
-        p = t % 2
-        if t >= 2:
-            ocp(t - 2, p).wait()
-        dxo[p] = dxa[t].astype(bf16)
-        ocp(t, p).start()
-    zown = pltpu.make_async_copy(zf, z_hbm.at[pl.ds(ci * 6, 6)], sg.at[0])
-    zoth = pltpu.make_async_copy(zr, z_hbm.at[pl.ds(6 - ci * 6, 6)], sg.at[1])
-    zown.start()
-    arrived(26, 27)
-    zoth.start()
-    for p in (0, 1):
-        for cp in outcp(n - 2 + p, p):
+    zown[1].start()
+    arrived(26)
+    zoth[0].start()
+    for q in (0, 1):
+        for cp in outs(n - 4 + 2 * q, q):
             cp.wait()
-    ocp(NT - 2, 0).wait()
-    ocp(NT - 1, 1).wait()
+        ocp(n - 4 + 2 * q, q, 0).wait()
+    ocp(n - 3, 1, 1).wait()
     for k in range(len(table)):
         rc(k).wait_send()
-    zown.wait()
-    zoth.wait()
+    arrived(27)
+    zoth[1].start()
+    ocp(n - 1, 0, 1).wait()
+    for cp in zown + zoth:
+        cp.wait()
 
 
 def call_a(x, dy, w1, w3, w2, g):
     part = (3, 2, 144, FB)
+    dma = pltpu.SemaphoreType.DMA
     return pl.pallas_call(
         kernel_a,
         out_shape=(jax.ShapeDtypeStruct((D, T), bf16), jax.ShapeDtypeStruct((3, F, T), bf16),
@@ -355,19 +372,14 @@
         in_specs=[ANY] * 6, out_specs=[ANY] * 3,
         scratch_shapes=[
             pltpu.VMEM((NT, D, TB), bf16), pltpu.VMEM((NT, D, TB), bf16),
-            pltpu.VMEM((2, 3, FB, TB), f32), pltpu.VMEM((2, 2 * FB, TB), bf16),
-            pltpu.VMEM((2, FB, TB), bf16), pltpu.VMEM((NT, D, TB), f32),
-            pltpu.VMEM((2, D, TB), bf16),
+            pltpu.VMEM((2, 3, FB, TB), f32), *[pltpu.VMEM((2, 2 * FB, TB), bf16)] * 2,
+            *[pltpu.VMEM((2, FB, TB), bf16)] * 2, pltpu.VMEM((NT, D, TB), f32),
+            *[pltpu.VMEM((2, D, TB), bf16)] * 2,
             pltpu.VMEM((NF, 3, FB, D), bf16), pltpu.VMEM((NF, D, 2 * FB), bf16),
-            pltpu.VMEM((2, 3, 144, F), f32), pltpu.VMEM((6, 144, F), bf16),
-            pltpu.VMEM((6, 144, F), bf16),
-            pltpu.VMEM(part, bf16), pltpu.VMEM(part, bf16), pltpu.VMEM(part, bf16),
-            pltpu.VMEM(part, bf16), pltpu.VMEM(part, bf16), pltpu.VMEM(part, bf16),
-            pltpu.VMEM((6, 144, FB), f32), pltpu.VMEM((6, 144, FB), f32),
-            pltpu.SemaphoreType.DMA((NT,)), pltpu.SemaphoreType.DMA((NT,)),
-            pltpu.SemaphoreType.DMA((2, 3)), pltpu.SemaphoreType.DMA((2,)),
-            pltpu.SemaphoreType.DMA((3,)), pltpu.SemaphoreType.DMA((2,)),
-            pltpu.SemaphoreType.DMA((28,)), pltpu.SemaphoreType.DMA((28,))],
+            pltpu.VMEM((2, 3, 144, F), f32), *[pltpu.VMEM((6, 144, F), bf16)] * 2,
+            *[pltpu.VMEM(part, bf16)] * 6, *[pltpu.VMEM((6, 144, FB), f32)] * 2,
+            dma((NT,)), dma((NT,)), dma((2, 2, 3)), dma((2, 2)), dma((3,)), dma((2,)),
+            dma((28,)), dma((28,))],
         compiler_params=pltpu.CompilerParams(vmem_limit_bytes=67043328, collective_id=0,
                                              has_side_effects=True),
         cost_estimate=pl.CostEstimate(flops=40_000_000_000, bytes_accessed=60_000_000,
@@ -375,30 +387,128 @@
         name="fwd_dx")(x, dy, w1, w3, w2, g)
 
 
-def kernel_b(x_ref, dy_ref, r_ref, o_ref):
-    m = pl.program_id(0)
-
-    @pl.when(m < 2)
-    def _():
-        o_ref[0] = lax.dot_general(x_ref[...], r_ref[0], NTD, preferred_element_type=f32)
-
-    @pl.when(m == 2)
-    def _():
-        o_ref[0] = lax.dot_general(dy_ref[...], r_ref[0], NTD, preferred_element_type=f32)
-
-
-def call_b(x, dy, r):
-    bn = 512
-    whole = pl.BlockSpec((D, T), lambda m, n: (0, 0), pipeline_mode=pl.Buffered(1))
+def kernel_b(x_hbm, dy_hbm, r_hbm, dxi_hbm, z_hbm, o_hbm, dx_hbm, n_hbm,
+             xy, r, o, dxb, zb, zt, sxk, srk, sdy, sr, so, sdx, sz, sn):
+    ci = lax.axis_index("fi") % 2
+    KC = T // 4
+
+    def xk(k):
+        return pltpu.make_async_copy(x_hbm.at[:, pl.ds(k * KC, KC)], xy.at[0, :, pl.ds(k * KC, KC)],
+                                     sxk.at[k])
+
+    def rk(k):
+        return pltpu.make_async_copy(r_hbm.at[0, pl.ds(0, BN), pl.ds(k * KC, KC)],
+                                     r.at[0, :, pl.ds(k * KC, KC)], srk.at[k])
+
+    def rcp(m, n):
+        return pltpu.make_async_copy(r_hbm.at[m, pl.ds(n * BN, BN), :], r.at[n], sr.at[n])
+
+    def ocp(m, n):
+        return pltpu.make_async_copy(o.at[n], o_hbm.at[m, :, pl.ds(n * BN, BN)], so.at[n])
+
+    def ncp(m):
+        return pltpu.make_async_copy(zt.at[m, pl.ds(pl.multiple_of(ci * 192, 192), 192), :],
+                                     n_hbm.at[m], sn.at[m])
+
+    dyc = pltpu.make_async_copy(dy_hbm, xy.at[1], sdy)
+    dxin = pltpu.make_async_copy(dxi_hbm, dxb, sdx.at[0])
+    dxout = pltpu.make_async_copy(dxb, dx_hbm, sdx.at[1])
+
+    def zcp(m):
+        return pltpu.make_async_copy(z_hbm.at[m], zb.at[m], sz.at[m])
+
+    for k in range(4):
+        xk(k).start()
+        rk(k).start()
+    rcp(0, 1).start()
+    zcp(0).start()
+    rcp(0, 2).start()
+    for k in range(4):
+        xk(k).wait()
+        rk(k).wait()
+        ks = slice(k * KC, (k + 1) * KC)
+        v = lax.dot_general(xy[0, :, ks], r[0, :, ks], NTD, preferred_element_type=f32)
+        o[0] = v if k == 0 else o[0] + v
+
+    def ready(m, n):
+        rcp(m, n).wait()
+
+        @pl.when(m > 0)
+        def _():
+            ocp(m - 1, n).wait()
+
+    def gw(m, n):
+        o[n] = lax.dot_general(xy[m // 2], r[n], NTD, preferred_element_type=f32)
+
+    def after(m, n):
+        ocp(m, n).start()
+
+        @pl.when(m < 2)
+        def _():
+            rcp(m + 1, n).start()
+
+    def block(m, c):
+        @pl.when(m == 2)
+        def _():
+            dyc.wait()
+            dxin.wait()
+            dxout.start()
+
+        @pl.when(m > 0)
+        def _():
+            ready(m, 0)
+            gw(m, 0)
+
+        after(m, 0)
+        ready(m, 1)
+        zcp(m).wait()
+        gw(m, 1)
+        zt[m] = zb[m].T
+        after(m, 1)
+        ncp(m).start()
+
+        @pl.when(m < 2)
+        def _():
+            zcp(m + 1).start()
+
+        @pl.when(m == 0)
+        def _():
+            dyc.start()
+
+        @pl.when(m == 1)
+        def _():
+            dxin.start()
+
+        ready(m, 2)
+        gw(m, 2)
+        after(m, 2)
+        return c
+
+    lax.fori_loop(0, 3, block, 0)
+    dxout.wait()
+    for m in range(3):
+        ncp(m).wait()
+        ocp(2, m).wait()
+
+
+BN = 512
+
+
+def call_b(x, dy, r, dxi, z):
+    dma = pltpu.SemaphoreType.DMA
     return pl.pallas_call(
         kernel_b,
-        out_shape=jax.ShapeDtypeStruct((3, D, F), f32), grid=(3, F // bn),
-        in_specs=[whole, whole, pl.BlockSpec((1, bn, T), lambda m, n: (m, n, 0))],
-        out_specs=pl.BlockSpec((1, D, bn), lambda m, n: (m, 0, n)),
+        out_shape=(jax.ShapeDtypeStruct((3, D, F), f32), jax.ShapeDtypeStruct((D, T), bf16),
+                   jax.ShapeDtypeStruct((3, 192, D), f32)),
+        in_specs=[ANY] * 5, out_specs=[ANY] * 3,
+        scratch_shapes=[
+            pltpu.VMEM((2, D, T), bf16), pltpu.VMEM((3, BN, T), bf16), pltpu.VMEM((3, D, BN), f32),
+            pltpu.VMEM((D, T), bf16), pltpu.VMEM((3, D, FB), f32), pltpu.VMEM((3, FB, D), f32),
+            dma((4,)), dma((4,)), dma, dma((3,)), dma((3,)), dma((2,)), dma((3,)), dma((3,))],
         compiler_params=pltpu.CompilerParams(vmem_limit_bytes=60 << 20),
         cost_estimate=pl.CostEstimate(flops=30_000_000_000, bytes_accessed=60_000_000,
                                       transcendentals=0),
-        name="wgrad")(x, dy, r)
+        name="wgrad")(x, dy, r, dxi, z)
 
 
 def solution(mesh):
@@ -407,9 +517,8 @@
 
     def local(x, dy, w1s, w3s, w2s, g):
         dx, r, z = call_a(x.T, dy.T, w1s.T, w3s.T, w2s, g.reshape(12, 144, F))
-        dwl = call_b(x.T, dy.T, r)
-        dwn = lax.dynamic_slice_in_dim(z.reshape(3, D, FB), lax.axis_index("fi") % 2 * 192, 192, 2)
-        return dx.T, dwn, dwl[None]
+        dwl, dx, dwn = call_b(x.T, dy.T, r, dx, z.reshape(3, D, FB))
+        return dx.T, dwn.transpose(0, 2, 1), dwl[None]
 
     return jax.shard_map(
         local, mesh=mesh,

time: 110 us -> 96.9 us (0.88)
  local copies, waits for them, and re-layouts: 9.1 us -> 0 us
  Pallas kernels: 99.9 us -> 96 us
    unnamed x2 -> x0, local copies, waits for them, and re-layouts: 6.82 us -> none
    dynamic_slice x1 -> x0, local copies, waits for them, and re-layouts: 2.28 us -> none  [local(): lax.dynamic_slice_in_dim(z.reshape(3, D, FB), lax.axis_index('fi') % 2 *...]
    pallas_call x1, Pallas kernels: 29.9 us -> 27.9 us  [call_b(): pl.pallas_call(kernel_b, out_shape=(jax.ShapeDtypeStruct((3, D, F), f32),...]
    pallas_call x1, Pallas kernels: 70 us -> 68.1 us  [call_a(): pl.pallas_call(kernel_a, out_shape=(jax.ShapeDtypeStruct((D, T), bf16), j...]
where the time goes in v3:
time: 96.9 us; the launch traced here: 96.8 us
  Pallas kernels  96 us (99%)
    pallas_call x1, Pallas kernels, call_a(): pl.pallas_call(kernel_a, out_shape=(jax.ShapeDtypeStruct((D, T), bf16), j...  68.1 us
    pallas_call x1, Pallas kernels, call_b(): pl.pallas_call(kernel_b, out_shape=(jax.ShapeDtypeStruct((3, D, F), f32),...  27.9 us

profile of v3, /device:TPU:0, one launch (start us, length us, event | category | flops | bytes accessed | tf_op | source)
XLA Modules:
  0.0 96.8 jit_solution(6716342682230028078)
XLA Ops:
  0.6 68.1 %fwd_dx.1 = (bf16[576,4096]{1,0:T(8,128)(2,1)}, bf16[3,1536,4096]{2,1,0:T(8,128)(2,1)}, f32[12,144,384]{2,1,0:T(8,128)}) custom-call(bf16[576,4096]{1,0:T(8,128)(2,1)} %bitcast.10, bf16[576,4096]{1,0:T(8,128)(2,1)} %bitcast.12, bf16[192,576]{1,0:T(8,128)(2,1)} %bitcast.14, bf16[192,576]{1,0:T(8,128)(2,1)} %bitcast.15, bf16[192,576]{1,0:T(8,128)(2,1)} %w2_hbm.1, ...), custom_call_target="tpu_custom_call" | custom-call | flops 40000000000 | bytes 60000000 | tf_op jit(solution)/shard_map/fwd_dx/pallas_call | solution.py:368
  68.7 27.9 %wgrad.1 = (f32[3,576,1536]{2,1,0:T(8,128)}, bf16[576,4096]{1,0:T(8,128)(2,1)}, f32[3,192,576]{2,1,0:T(8,128)}) custom-call(bf16[576,4096]{1,0:T(8,128)(2,1)} %bitcast.11, bf16[576,4096]{1,0:T(8,128)(2,1)} %bitcast.13, bf16[3,1536,4096]{2,1,0:T(8,128)(2,1)} %get-tuple-element.9.r_hbm, bf16[576,4096]{1,0:T(8,128)(2,1)} %get-tuple-element.10.dxi_hbm, ...), custom_call_target="tpu_custom_call" | custom-call | flops 30000001024 | bytes 60000000 | tf_op jit(solution)/shard_map/wgrad/pallas_call | solution.py:499

commit v4 on v3

v4 whole, which is shorter than its diff:
```python
import jax
import jax.numpy as jnp
from jax import lax
from jax.experimental import pallas as pl
from jax.experimental.pallas import tpu as pltpu
from jax.sharding import PartitionSpec as P

bf16, f32 = jnp.bfloat16, jnp.float32
T, D, F = 4096, 576, 1536
FB, TB, RC = 384, 512, 16
NF, NT = F // FB, T // TB
NN = (((1,), (0,)), ((), ()))
NTD = (((1,), (1,)), ((), ()))
ANY = pl.BlockSpec(memory_space=pl.ANY)
VM = pl.BlockSpec(memory_space=pltpu.VMEM)


def dot(a, b):
    return lax.dot_general(a, b, NN, preferred_element_type=f32)


def kernel_a(x_hbm, dy_hbm, w1_hbm, w3_hbm, w2_hbm, g_hbm, dx_hbm, r_hbm, z_hbm, og_hbm,
             x, dy, acts, dda, ddb, dxa, dxoa, dxob, wg, wd, gst, sb, rb, r0, r1, r2,
             qb, fin, rz, zf, zr,
             sx, sd, so, sdx, sw, sg, ssem, rsem):
    dd, dxo = (dda, ddb), (dxoa, dxob)
    zi, yi, fi = lax.axis_index("dp"), lax.axis_index("fo"), lax.axis_index("fi")
    xi, ci = fi // 2, fi % 2
    to_c = (zi, yi, xi * 2 + 1 - ci)
    to_x = (zi, yi, (1 - xi) * 2 + ci)
    to_y = (zi, 1 - yi, fi)
    to_z = (1 - zi, yi, fi)
    own = ci * 192
    half, other = own + zi * 96, own + (1 - zi) * 96

    def blk(yy, xx):
        return pl.ds(pl.multiple_of((yy * 2 + xx) * FB, FB), FB)

    def wrows(j, r, n):
        return wg.at[j, :, pl.ds(pl.multiple_of(r, 16), n), :]

    def piece(k, yy, xx):
        return rb.at[pl.ds(2 * k, 2), :, blk(yy, xx)]

    table = [
        (wrows(0, own, 192), wrows(0, own, 192), to_c),
        (wrows(0, own, 192), wrows(1, own, 192), to_x),
        (wrows(0, half, 96), wrows(2, half, 96), to_y),
        (wrows(1, own, 192), wrows(1, own, 192), to_c),
        (wrows(2, half, 96), wrows(2, half, 96), to_z),
        (wrows(2, half, 96), wrows(2, half, 96), to_c),
        (wrows(2, other, 96), wrows(2, other, 96), to_c),
        (wrows(1, half, 48), wrows(3, half, 48), to_y),
        (wrows(2, half + 48, 48), wrows(3, half + 48, 48), to_x),
        (wrows(3, half, 96), wrows(3, half, 96), to_z),
        (wrows(3, half, 96), wrows(3, half, 96), to_c),
        (wrows(3, other, 96), wrows(3, other, 96), to_c),
    ]
    yo, xo = 1 - yi, 1 - xi
    fst, snd = (to_y, to_y, to_x), (to_x, to_x, to_y)
    far, near = ((yi, xo), (yi, xo), (yo, xi)), ((yo, xi), (yo, xi), (yi, xo))
    zp = (pl.ds(0, 4), pl.ds(4, 2))
    table += [(sb.at[pl.ds(k, 3)], rb.at[pl.ds(k, 3)], to_c) for k in (0, 3)]
    table += [(piece(k, yo, xo), r0.at[k], fst[k]) for k in range(3)]
    table += [(piece(k, *near[k]), r1.at[k], fst[k]) for k in range(3)]
    table += [(qb.at[k], r2.at[k], snd[k]) for k in range(3)]
    table += [(fin.at[k], rz.at[k], to_z) for k in range(3)]
    table += [(zf.at[sl], zr.at[sl], to_c) for sl in zp]

    def rc(k):
        src, dst, dev = table[k]
        return pltpu.make_async_remote_copy(src, dst, ssem.at[k], rsem.at[k], device_id=dev,
                                            device_id_type=pl.DeviceIdType.MESH)

    def start(*ks):
        for k in ks:
            rc(k).start()

    def arrived(*ks):
        for k in ks:
            rc(k).wait_recv()

    def xcp(t):
        return pltpu.make_async_copy(x_hbm.at[:, pl.ds(t * TB, TB)], x.at[t], sx.at[t])

    def dcp(t):
        return pltpu.make_async_copy(dy_hbm.at[:, pl.ds(t * TB, TB)], dy.at[t], sd.at[t])

    def gcp(i, side):
        return pltpu.make_async_copy(g_hbm.at[pl.ds(side * 6 + i * 3, 3)], gst.at[pl.ds(i * 3, 3)], sg.at[i])

    wcps = [pltpu.make_async_copy(h, wg.at[0, m, pl.ds(pl.multiple_of(own, 192), 192), :], sw.at[m])
            for m, h in enumerate((w1_hbm, w3_hbm, w2_hbm))]
    for cp in wcps:
        cp.start()
    bar = pltpu.get_barrier_semaphore()
    for dev in (to_c, to_x, to_y, to_z):
        pl.semaphore_signal(bar, inc=1, device_id=dev, device_id_type=pl.DeviceIdType.MESH)
    xcp(0).start()
    dcp(0).start()
    xcp(1).start()
    dcp(1).start()
    for i in (0, 1):
        gcp(i, 1 - ci).start()
    for t in range(2, NT):
        xcp(t).start()
        dcp(t).start()
    ddb[3] = jnp.zeros(ddb.shape[1:], bf16)
    for cp in wcps:
        cp.wait()
    pl.semaphore_wait(bar, 4)
    start(0, 1, 2)

    def flip(j):
        for m in (0, 1):
            wd[j, :, m * FB:(m + 1) * FB] = wg[j, m].T

    def outs(s0, q, first=False):
        j = s0 // NT
        yj = yi + (j // 2) * (1 - 2 * yi)
        xj = xi + (j % 2) * (1 - 2 * xi)
        fs = blk(yj, xj)
        w, m = (s0 // 2, 2) if first else (q, slice(None))
        return [pltpu.make_async_copy(
            dd[p].at[w, m], r_hbm.at[m, fs, pl.ds(pl.multiple_of((s0 + p) % NT * TB, TB), TB)],
            so.at[w, p]) for p in (0, 1)]

    def fwd(f, t, p):
        acts[p, 0] = dot(wg[f, 0], x[t])
        acts[p, 1] = dot(wg[f, 1], x[t])
        acts[p, 2] = dot(wg[f, 2], dy[t])

    def ew(p, w):
        for r in range(0, FB, RC):
            a, b, dh = (acts[p, k, r:r + RC, :] for k in range(3))
            s = 0.5 * jnp.tanh(0.5 * a) + 0.5
            sa = a * s
            dd[p][w, 2, r:r + RC, :] = (sa * b).astype(bf16)
            dd[p][w, 0, r:r + RC, :] = (dh * b * (s * (1.0 + a * (1.0 - s)))).astype(bf16)
            dd[p][w, 1, r:r + RC, :] = (dh * sa).astype(bf16)

    def ocp(s, q, p):
        ts = pl.ds(pl.multiple_of(s % NT * TB, TB), TB)
        return pltpu.make_async_copy(dxo[p].at[q], dx_hbm.at[:, ts], sdx.at[q, p])

    def dab(p, w):
        return dd[p][w, :2].reshape(2 * FB, TB)

    def dxp(s, q, p, first, o=None):
        t = s % NT
        if first:
            dxa[t] = dot(wd[0], dab(p, q))
            return
        v = dxa[t] + dot(wd[s // NT], dab(p, q))
        dxa[t] = v
        if o is not None:
            dxo[p][o] = v.astype(bf16)

    def tiles(i, first, extra=None, last=False):
        s0, q = 2 * i, i % 2
        w = i if first else q
        prev = (i + 3) % 4 if first else 1 - q if last else 1 - q + 2 * ((11 - i) // 7)
        f, t0 = s0 // NT, s0 % NT

        if not first:
            @pl.when(i > 5)
            def _():
                for cp in outs(s0 - 4, q):
                    cp.wait()

        if last:
            @pl.when(i > 13)
            def _():
                ocp(s0 - 5, q, 1).wait()
                ocp(s0 - 4, q, 0).wait()

        o = q if last else None
        fwd(f, t0, 0)
        ew(0, w)
        if extra is not None:
            extra(0)
        dxp(s0 + NT - 1 if first else s0 - 1, prev, 1, first, o)
        fwd(f, t0 + 1, 1)
        ew(1, w)
        if extra is not None:
            extra(1)
        dxp(s0, w, 0, first, o)
        for cp in outs(s0, q, first):
            cp.start()
        if last:
            ocp(s0 - 1, q, 1).start()
            ocp(s0, q, 0).start()

    def need(i):
        for t in (2 * i, 2 * i + 1):
            xcp(t).wait()
            dcp(t).wait()

    def phase0a(i, c):
        need(i)
        gcp(i, 1 - ci).wait()

        def conv(h):
            for gr in range(3):
                for r in range(72 * h, 72 * h + 72, 24):
                    sb[i * 3 + gr, r:r + 24, :] = gst[i * 3 + gr, r:r + 24, :].astype(bf16)

        tiles(i, True, conv)

        @pl.when(i == 0)
        def _():
            start(12)

        @pl.when(i == 1)
        def _():
            start(13)

        gcp(i, ci).start()
        return c

    def phase0b(i, c):
        need(i + 2)
        gcp(i, ci).wait()

        @pl.when(i == 0)
        def _():
            arrived(12)

        @pl.when(i == 1)
        def _():
            arrived(13)
            start(14)
            arrived(2)
            start(4, 5, 8)

        def conv(h):
            for gr in range(3):
                for r in range(72 * h, 72 * h + 72, 24):
                    v = gst[i * 3 + gr, r:r + 24, :].astype(bf16).astype(f32)
                    v = v + rb[i * 3 + gr, r:r + 24, :].astype(f32)
                    rb[i * 3 + gr, r:r + 24, :] = v.astype(bf16)

        tiles(i + 2, True, conv)
        return c

    arrived(0)
    flip(0)
    lax.fori_loop(0, 2, phase0a, 0)
    lax.fori_loop(0, 2, phase0b, 0)
    start(15, 16)
    def own_grads(ts):
        return sum(lax.dot_general(x[t], dab(t % 2, t // 2), NTD, preferred_element_type=f32)
                   for t in ts).reshape(4, 144, 2 * FB)

    og = gst.at[pl.ds(0, 4), :, pl.ds(0, 2 * FB)]
    og[...] = own_grads(range(4))
    arrived(1)
    start(3, 7)
    og[...] += own_grads(range(4, NT))
    ogc = pltpu.make_async_copy(og, og_hbm, sw.at[2])
    ogc.start()
    for i in range(NT // 2):
        for cp in outs(2 * i, 0, True):
            cp.wait()
    arrived(3)
    flip(1)
    start(17, 18)

    def relay(k):
        qb[k] = (rb[2 * k:2 * k + 2, :, blk(*far[k])].astype(f32) + r0[k].astype(f32)).astype(bf16)

    def group_sum(k):
        fin[k] = (rb[2 * k:2 * k + 2, :, blk(yi, xi)].astype(f32) + r1[k].astype(f32)
                  + r2[k].astype(f32)).astype(bf16)

    def total(k):
        zf[2 * k:2 * k + 2] = fin[k].astype(f32) + rz[k].astype(f32)

    def at5():
        arrived(14)
        relay(0)
        start(20)
        arrived(4)
        start(6)

    def at6():
        arrived(15)
        relay(1)
        start(21)

    def at7():
        arrived(7, 8)
        start(9, 10)
        arrived(16)
        relay(2)
        start(22, 19)

    def at8():
        arrived(5, 6)
        flip(2)

    def at10():
        arrived(17, 20)
        group_sum(0)
        start(23)

    def at11():
        arrived(18, 21)
        group_sum(1)
        start(24)
        arrived(9)
        start(11)

    def at12():
        arrived(10, 11)
        flip(3)
        arrived(19, 22)
        group_sum(2)
        start(25)

    def zown(q):
        sl = zp[q]
        return pltpu.make_async_copy(zf.at[sl], z_hbm.at[pl.ds(ci * 6 + sl.start, sl.size)], sg.at[q])

    def at15():
        arrived(23, 24)
        total(0)
        total(1)
        start(26)
        zown(0).start()

    events = {5: at5, 6: at6, 7: at7, 8: at8, 10: at10, 11: at11}

    def phase1(i, c):
        for k, ev in events.items():
            pl.when(i == k)(ev)
        tiles(i, False)
        return c

    def phase2(i, c):
        pl.when(i == 15)(at15)
        tiles(i, False, last=True)
        return c

    n = NF * NT
    lax.fori_loop(NT // 2, 12, phase1, 0)
    at12()
    lax.fori_loop(12, n // 2, phase2, 0)
    ocp(n - 5, 0, 1).wait()
    dxp(n - 1, 1, 1, False, 0)
    ocp(n - 1, 0, 1).start()
    zoth = [pltpu.make_async_copy(zr.at[sl], z_hbm.at[pl.ds(6 - ci * 6 + sl.start, sl.size)], sw.at[q])
            for q, sl in enumerate(zp)]
    arrived(25)
    total(2)
    start(27)
    zown(1).start()
    arrived(26)
    zoth[0].start()
    for q in (0, 1):
        for cp in outs(n - 4 + 2 * q, q):
            cp.wait()
        ocp(n - 4 + 2 * q, q, 0).wait()
    ocp(n - 3, 1, 1).wait()
    for k in range(len(table)):
        rc(k).wait_send()
    arrived(27)
    zoth[1].start()
    ocp(n - 1, 0, 1).wait()
    for cp in zoth + [zown(0), zown(1), ogc]:
        cp.wait()


def call_a(x, dy, w1, w3, w2, g):
    part = (3, 2, 144, FB)
    dma = pltpu.SemaphoreType.DMA
    return pl.pallas_call(
        kernel_a,
        out_shape=(jax.ShapeDtypeStruct((D, T), bf16), jax.ShapeDtypeStruct((3, F, T), bf16),
                   jax.ShapeDtypeStruct((12, 144, FB), f32),
                   jax.ShapeDtypeStruct((4, 144, 2 * FB), f32)),
        in_specs=[ANY] * 6, out_specs=[ANY] * 4,
        scratch_shapes=[
            pltpu.VMEM((NT, D, TB), bf16), pltpu.VMEM((NT, D, TB), bf16),
            pltpu.VMEM((2, 3, FB, TB), f32), *[pltpu.VMEM((4, 3, FB, TB), bf16)] * 2,
            pltpu.VMEM((NT, D, TB), f32),
            *[pltpu.VMEM((2, D, TB), bf16)] * 2,
            pltpu.VMEM((NF, 3, FB, D), bf16), pltpu.VMEM((NF, D, 2 * FB), bf16),
            pltpu.VMEM((6, 144, F), f32), *[pltpu.VMEM((6, 144, F), bf16)] * 2,
            *[pltpu.VMEM(part, bf16)] * 6, *[pltpu.VMEM((6, 144, FB), f32)] * 2,
            dma((NT,)), dma((NT,)), dma((4, 2)), dma((2, 2)), dma((3,)), dma((2,)),
            dma((28,)), dma((28,))],
        compiler_params=pltpu.CompilerParams(vmem_limit_bytes=67043328, collective_id=0,
                                             has_side_effects=True),
        name="fwd_dx")(x, dy, w1, w3, w2, g)


def kernel_b(x_hbm, dy_hbm, r_hbm, dxi_hbm, z_hbm, og_hbm, o_hbm, dx_hbm, n_hbm,
             xy, r0, r, o0, o, dxb, ogb, zb, zt, sx, s0, so0, sdy, sr, so, sdx, sog, sz, sn):
    yi, fi = lax.axis_index("fo"), lax.axis_index("fi")
    xi, ci = fi // 2, fi % 2

    def cols(b, n):
        return pl.ds(pl.multiple_of(b * n, n), n)

    def tri(src, dst, sem):
        return pltpu.make_async_copy(src, dst, sem)

    nb = cols(yi * 2 + 1 - xi, FB)
    mine = cols(yi * 2 + xi, FB)
    ks = [pl.ds(k * KC, KC) for k in range(T // KC)]
    first = [[tri(x_hbm.at[:, k], xy.at[0, :, k], sx.at[q])]
             + [tri(r_hbm.at[m, nb, k], r0.at[pl.ds(m * FB, FB), k], s0.at[m, q]) for m in (0, 1)]
             for q, k in enumerate(ks)]
    o0c = [tri(o0.at[:, pl.ds(m * FB, FB)], o_hbm.at[m, :, nb], so0.at[m]) for m in (0, 1)]
    dyc = tri(dy_hbm, xy.at[1], sdy)
    dxin, dxout = tri(dxi_hbm, dxb, sdx.at[0]), tri(dxb, dx_hbm, sdx.at[1])
    ogin = tri(og_hbm, ogb, sog.at[2])
    ogout = [tri(ogb.at[:, pl.ds(m * FB, FB)], o_hbm.at[m, :, mine], sog.at[m]) for m in (0, 1)]

    def place(s):
        return s - s // 3, cols((1 - s // 2) * (1 - yi) + s // 3, BN)

    def rcp(s):
        m, c = place(s)
        return tri(r_hbm.at[m, c, :], r.at[s % 2], sr.at[s % 2])

    def ocp(s):
        m, c = place(s)
        return tri(o.at[s % 2], o_hbm.at[m, :, c], so.at[s % 2])

    def zcp(m):
        return tri(z_hbm.at[m], zb.at[m], sz.at[m])

    def ncp(m):
        return tri(zt.at[m, cols(ci, FB // 2), :], n_hbm.at[m], sn.at[m])

    for cps in first:
        for cp in cps:
            cp.start()
    rcp(0).start()
    rcp(1).start()
    for m in range(3):
        zcp(m).start()
    dyc.start()
    zb[3] = jnp.zeros(zb.shape[1:], f32)
    for q, cps in enumerate(first):
        for cp in cps:
            cp.wait()
        v = lax.dot_general(xy[0, :, ks[q]], r0[:, ks[q]], NTD, preferred_element_type=f32)
        o0[...] = v if q == 0 else o0[...] + v
    for cp in o0c:
        cp.start()

    def step(s, c):
        pl.when(s == 2)(dyc.wait)

        @pl.when(s == 3)
        def _():
            dxin.wait()
            dxout.start()
            ogin.wait()
            for cp in ogout:
                cp.start()

        @pl.when(s > 0)
        def _():
            zcp(s - 1).wait()

        rcp(s).wait()
        pl.when(s > 1)(ocp(s - 2).wait)
        o[s % 2] = lax.dot_general(xy[s // 2], r[s % 2], NTD, preferred_element_type=f32)
        zt[(s + 3) % 4] = zb[(s + 3) % 4].T
        ocp(s).start()

        @pl.when(s > 0)
        def _():
            ncp(s - 1).start()

        @pl.when(s < 2)
        def _():
            rcp(s + 2).start()

        pl.when(s == 0)(dxin.start)
        pl.when(s == 1)(ogin.start)
        return c

    lax.fori_loop(0, 4, step, 0)
    for cp in o0c + ogout + [dxout, ocp(2), ocp(3)] + [ncp(m) for m in range(3)]:
        cp.wait()


BN, KC = 2 * FB, 1024


def call_b(x, dy, r, dxi, z, og):
    dma = pltpu.SemaphoreType.DMA
    return pl.pallas_call(
        kernel_b,
        out_shape=(jax.ShapeDtypeStruct((3, D, F), f32), jax.ShapeDtypeStruct((D, T), bf16),
                   jax.ShapeDtypeStruct((3, FB // 2, D), f32)),
        in_specs=[ANY] * 6, out_specs=[ANY] * 3,
        scratch_shapes=[
            pltpu.VMEM((2, D, T), bf16), pltpu.VMEM((BN, T), bf16), pltpu.VMEM((2, BN, T), bf16),
            pltpu.VMEM((D, BN), f32), pltpu.VMEM((2, D, BN), f32), pltpu.VMEM((D, T), bf16),
            pltpu.VMEM((D, BN), f32), pltpu.VMEM((4, D, FB), f32), pltpu.VMEM((4, FB, D), f32),
            dma((4,)), dma((2, 4)), dma((2,)), dma, dma((2,)), dma((2,)), dma((2,)), dma((3,)),
            dma((3,)), dma((3,))],
        compiler_params=pltpu.CompilerParams(vmem_limit_bytes=60 << 20),
        name="wgrad")(x, dy, r, dxi, z, og)


def solution(mesh):
    grp = ("fo", "fi")
    alla = ("dp", "fo", "fi")

    def local(x, dy, w1s, w3s, w2s, g):
        dx, r, z, og = call_a(x.T, dy.T, w1s.T, w3s.T, w2s, g.reshape(12, 144, F))
        dwl, dx, dwn = call_b(x.T, dy.T, r, dx, z.reshape(3, D, FB), og.reshape(D, BN))
        return dx.T, dwn.transpose(0, 2, 1), dwl[None]

    return jax.shard_map(
        local, mesh=mesh,
        in_specs=(P(alla, None), P(alla, None), P(None, grp), P(None, grp), P(grp, None),
                  P(alla, None, None, None)),
        out_specs=(P(alla, None), P(None, None, grp), P(alla, None, None, None)),
        check_vma=False)
```

time: 96.9 us -> 94.7 us (0.977)
  Pallas kernels: 96 us -> 93.8 us
    pallas_call x1, Pallas kernels: 27.9 us -> 25.2 us  [call_b(): pl.pallas_call(kernel_b, out_shape=(jax.ShapeDtypeStruct((3, D, F), f32),...]
where the time goes in v4:
time: 94.7 us; the launch traced here: 94.6 us
  Pallas kernels  93.8 us (99%)
    pallas_call x1, Pallas kernels, call_a(): pl.pallas_call(kernel_a, out_shape=(jax.ShapeDtypeStruct((D, T), bf16), j...  68.6 us
    pallas_call x1, Pallas kernels, call_b(): pl.pallas_call(kernel_b, out_shape=(jax.ShapeDtypeStruct((3, D, F), f32),...  25.2 us

profile of v4, /device:TPU:0, one launch (start us, length us, event | category | flops | bytes accessed | tf_op | source)
XLA Modules:
  0.0 94.6 jit_solution(6537749439693805955)
XLA Ops:
  0.6 68.6 %fwd_dx.1 = (bf16[576,4096]{1,0:T(8,128)(2,1)}, bf16[3,1536,4096]{2,1,0:T(8,128)(2,1)}, f32[12,144,384]{2,1,0:T(8,128)}, f32[4,144,768]{2,1,0:T(8,128)}) custom-call(bf16[576,4096]{1,0:T(8,128)(2,1)} %bitcast.10, bf16[576,4096]{1,0:T(8,128)(2,1)} %bitcast.12, bf16[192,576]{1,0:T(8,128)(2,1)} %bitcast.17, bf16[192,576]{1,0:T(8,128)(2,1)} %bitcast.18, ...), custom_call_target="tpu_custom_call" | custom-call | tf_op jit(solution)/shard_map/fwd_dx/pallas_call | solution.py:377
  69.2 25.2 %wgrad.1 = (f32[3,576,1536]{2,1,0:T(8,128)}, bf16[576,4096]{1,0:T(8,128)(2,1)}, f32[3,192,576]{2,1,0:T(8,128)}) custom-call(bf16[576,4096]{1,0:T(8,128)(2,1)} %bitcast.11, bf16[576,4096]{1,0:T(8,128)(2,1)} %bitcast.13, bf16[3,1536,4096]{2,1,0:T(8,128)(2,1)} %get-tuple-element.10.r_hbm, bf16[576,4096]{1,0:T(8,128)(2,1)} %get-tuple-element.11.dxi_hbm, ...), custom_call_target="tpu_custom_call" | custom-call | tf_op jit(solution)/shard_map/wgrad/pallas_call | solution.py:498

commit v5 on v4

--- a/solution.py
+++ b/solution.py
@@ -20,7 +20,7 @@
 
 
 def kernel_a(x_hbm, dy_hbm, w1_hbm, w3_hbm, w2_hbm, g_hbm, dx_hbm, r_hbm, z_hbm, og_hbm,
-             x, dy, acts, dda, ddb, dxa, dxoa, dxob, wg, wd, gst, sb, rb, r0, r1, r2,
+             x, dy, acts, dda, ddb, dxa, dxoa, dxob, wg, gst, sb, rb, r0, r1, r2,
              qb, fin, rz, zf, zr,
              sx, sd, so, sdx, sw, sg, ssem, rsem):
     dd, dxo = (dda, ddb), (dxoa, dxob)
@@ -111,10 +111,6 @@
     pl.semaphore_wait(bar, 4)
     start(0, 1, 2)
 
-    def flip(j):
-        for m in (0, 1):
-            wd[j, :, m * FB:(m + 1) * FB] = wg[j, m].T
-
     def outs(s0, q, first=False):
         j = s0 // NT
         yj = yi + (j // 2) * (1 - 2 * yi)
@@ -143,15 +139,19 @@
         ts = pl.ds(pl.multiple_of(s % NT * TB, TB), TB)
         return pltpu.make_async_copy(dxo[p].at[q], dx_hbm.at[:, ts], sdx.at[q, p])
 
+    def tdot(j, b):
+        return lax.dot_general(wg[j, :2].reshape(2 * FB, D), b, (((0,), (0,)), ((), ())),
+                               preferred_element_type=f32)
+
     def dab(p, w):
         return dd[p][w, :2].reshape(2 * FB, TB)
 
     def dxp(s, q, p, first, o=None):
         t = s % NT
         if first:
-            dxa[t] = dot(wd[0], dab(p, q))
+            dxa[t] = tdot(0, dab(p, q))
             return
-        v = dxa[t] + dot(wd[s // NT], dab(p, q))
+        v = dxa[t] + tdot(s // NT, dab(p, q))
         dxa[t] = v
         if o is not None:
             dxo[p][o] = v.astype(bf16)
@@ -244,7 +244,6 @@
         return c
 
     arrived(0)
-    flip(0)
     lax.fori_loop(0, 2, phase0a, 0)
     lax.fori_loop(0, 2, phase0b, 0)
     start(15, 16)
@@ -263,7 +262,6 @@
         for cp in outs(2 * i, 0, True):
             cp.wait()
     arrived(3)
-    flip(1)
     start(17, 18)
 
     def relay(k):
@@ -297,7 +295,6 @@
 
     def at8():
         arrived(5, 6)
-        flip(2)
 
     def at10():
         arrived(17, 20)
@@ -313,7 +310,6 @@
 
     def at12():
         arrived(10, 11)
-        flip(3)
         arrived(19, 22)
         group_sum(2)
         start(25)
@@ -385,7 +381,7 @@
             pltpu.VMEM((2, 3, FB, TB), f32), *[pltpu.VMEM((4, 3, FB, TB), bf16)] * 2,
             pltpu.VMEM((NT, D, TB), f32),
             *[pltpu.VMEM((2, D, TB), bf16)] * 2,
-            pltpu.VMEM((NF, 3, FB, D), bf16), pltpu.VMEM((NF, D, 2 * FB), bf16),
+            pltpu.VMEM((NF, 3, FB, D), bf16),
             pltpu.VMEM((6, 144, F), f32), *[pltpu.VMEM((6, 144, F), bf16)] * 2,
             *[pltpu.VMEM(part, bf16)] * 6, *[pltpu.VMEM((6, 144, FB), f32)] * 2,
             dma((NT,)), dma((NT,)), dma((4, 2)), dma((2, 2)), dma((3,)), dma((2,)),

time: 94.7 us -> 94.1 us (level)
  no operation moved by 1% of the time
where the time goes in v5:
time: 94.1 us; the launch traced here: 94 us
  Pallas kernels  93.2 us (99%)
    pallas_call x1, Pallas kernels, call_a(): pl.pallas_call(kernel_a, out_shape=(jax.ShapeDtypeStruct((D, T), bf16), j...  68 us
    pallas_call x1, Pallas kernels, call_b(): pl.pallas_call(kernel_b, out_shape=(jax.ShapeDtypeStruct((3, D, F), f32),...  25.2 us

profile of v5, /device:TPU:0, one launch (start us, length us, event | category | flops | bytes accessed | tf_op | source)
XLA Modules:
  0.0 94.0 jit_solution(8661283461975661808)
XLA Ops:
  0.6 68.0 %fwd_dx.1 = (bf16[576,4096]{1,0:T(8,128)(2,1)}, bf16[3,1536,4096]{2,1,0:T(8,128)(2,1)}, f32[12,144,384]{2,1,0:T(8,128)}, f32[4,144,768]{2,1,0:T(8,128)}) custom-call(bf16[576,4096]{1,0:T(8,128)(2,1)} %bitcast.10, bf16[576,4096]{1,0:T(8,128)(2,1)} %bitcast.12, bf16[192,576]{1,0:T(8,128)(2,1)} %bitcast.17, bf16[192,576]{1,0:T(8,128)(2,1)} %bitcast.18, ...), custom_call_target="tpu_custom_call" | custom-call | tf_op jit(solution)/shard_map/fwd_dx/pallas_call | solution.py:373
  68.7 25.2 %wgrad.1 = (f32[3,576,1536]{2,1,0:T(8,128)}, bf16[576,4096]{1,0:T(8,128)(2,1)}, f32[3,192,576]{2,1,0:T(8,128)}) custom-call(bf16[576,4096]{1,0:T(8,128)(2,1)} %bitcast.11, bf16[576,4096]{1,0:T(8,128)(2,1)} %bitcast.13, bf16[3,1536,4096]{2,1,0:T(8,128)(2,1)} %get-tuple-element.10.r_hbm, bf16[576,4096]{1,0:T(8,128)(2,1)} %get-tuple-element.11.dxi_hbm, ...), custom_call_target="tpu_custom_call" | custom-call | tf_op jit(solution)/shard_map/wgrad/pallas_call | solution.py:494

commit v6 on v5

--- a/solution.py
+++ b/solution.py
@@ -91,11 +91,11 @@
 
     wcps = [pltpu.make_async_copy(h, wg.at[0, m, pl.ds(pl.multiple_of(own, 192), 192), :], sw.at[m])
             for m, h in enumerate((w1_hbm, w3_hbm, w2_hbm))]
-    for cp in wcps:
-        cp.start()
     bar = pltpu.get_barrier_semaphore()
     for dev in (to_c, to_x, to_y, to_z):
         pl.semaphore_signal(bar, inc=1, device_id=dev, device_id_type=pl.DeviceIdType.MESH)
+    for cp in wcps:
+        cp.start()
     xcp(0).start()
     dcp(0).start()
     xcp(1).start()
@@ -109,7 +109,7 @@
     for cp in wcps:
         cp.wait()
     pl.semaphore_wait(bar, 4)
-    start(0, 1, 2)
+    start(1, 2, 0)
 
     def outs(s0, q, first=False):
         j = s0 // NT

time: 94.1 us -> 97.8 us (1.039)
  Pallas kernels: 93.2 us -> 96.9 us
    pallas_call x1, Pallas kernels: 68 us -> 71.7 us  [call_a(): pl.pallas_call(kernel_a, out_shape=(jax.ShapeDtypeStruct((D, T), bf16), j...]
where the time goes in v6:
time: 97.8 us; the launch traced here: 97.7 us
  Pallas kernels  96.9 us (99%)
    pallas_call x1, Pallas kernels, call_a(): pl.pallas_call(kernel_a, out_shape=(jax.ShapeDtypeStruct((D, T), bf16), j...  71.7 us
    pallas_call x1, Pallas kernels, call_b(): pl.pallas_call(kernel_b, out_shape=(jax.ShapeDtypeStruct((3, D, F), f32),...  25.2 us

profile of v6, /device:TPU:0, one launch (start us, length us, event | category | flops | bytes accessed | tf_op | source)
XLA Modules:
  0.0 97.7 jit_solution(16345025547942938905)
XLA Ops:
  0.6 71.7 %fwd_dx.1 = (bf16[576,4096]{1,0:T(8,128)(2,1)}, bf16[3,1536,4096]{2,1,0:T(8,128)(2,1)}, f32[12,144,384]{2,1,0:T(8,128)}, f32[4,144,768]{2,1,0:T(8,128)}) custom-call(bf16[576,4096]{1,0:T(8,128)(2,1)} %bitcast.10, bf16[576,4096]{1,0:T(8,128)(2,1)} %bitcast.12, bf16[192,576]{1,0:T(8,128)(2,1)} %bitcast.17, bf16[192,576]{1,0:T(8,128)(2,1)} %bitcast.18, ...), custom_call_target="tpu_custom_call" | custom-call | tf_op jit(solution)/shard_map/fwd_dx/pallas_call | solution.py:373
  72.3 25.2 %wgrad.1 = (f32[3,576,1536]{2,1,0:T(8,128)}, bf16[576,4096]{1,0:T(8,128)(2,1)}, f32[3,192,576]{2,1,0:T(8,128)}) custom-call(bf16[576,4096]{1,0:T(8,128)(2,1)} %bitcast.11, bf16[576,4096]{1,0:T(8,128)(2,1)} %bitcast.13, bf16[3,1536,4096]{2,1,0:T(8,128)(2,1)} %get-tuple-element.10.r_hbm, bf16[576,4096]{1,0:T(8,128)(2,1)} %get-tuple-element.11.dxi_hbm, ...), custom_call_target="tpu_custom_call" | custom-call | tf_op jit(solution)/shard_map/wgrad/pallas_call | solution.py:494
